TPU v7x, 256 devices: a whole 4x4x8 slice. The times are simulated.
256 devices in a mesh: dp: 32 (over z_lo, x, core), mp: 8 (over z_hi, y).
Axes of the slice: x: 4, y: 4, z: 8 (z_hi: 2, z_lo: 4; z = z_hi * 4 + z_lo), core: 2. Of those that a mesh axis runs over, the one named last changes fastest.
Arguments:
- queries: bfloat16 [24576, 1024], P('dp', 'mp'), may hold values from -3 to 3
- passages: bfloat16 [24576, 1024], P('dp', 'mp'), may hold values from -3 to 3
- positive: int32 [24576], P('dp'), may hold values from 0 to 24575
Outputs:
- grad_queries: bfloat16 [24576, 1024], P('dp', 'mp')
- grad_passages: bfloat16 [24576, 1024], P('dp', 'mp')
All inputs are finite; a program needn't handle non-finite values.
Results may differ from a plain program's by a relative error of at most 0.0034.
Values may be sent and summed in bfloat16 or wider, within the bound.
No kernel may reach another device: no remote copies, remote signals or barrier semaphores. Data moves between devices by JAX's collectives and lax.ppermute only.
A program may use at most 128 MiB of HBM per device.

v0:
```python
import functools
import math

import jax
import jax.numpy as jnp
from jax import lax
from jax.experimental import pallas as pl
from jax.experimental.pallas import tpu as pltpu
from jax.sharding import Mesh
from jax.sharding import PartitionSpec as P

WIDTH = ("zh", "y")
PLANE = ("x", "y")
F32, BF16 = jnp.float32, jnp.bfloat16
INTERPRET = False


def along_z(array, step):
    place = lambda z: (z % 4) * 2 + z // 4
    return lax.ppermute(array, ("zl", "zh"), [(place(z), place((z + step) % 8)) for z in range(8)])


def along(array, axis, step):
    return lax.ppermute(array, axis, [(k, (k + step) % 4) for k in range(4)])


def swapped(array, axis):
    return lax.ppermute(array, axis, [(0, 1), (1, 0)])


def to_plane(array):
    copies = jnp.broadcast_to(array[None], (16, *array.shape))
    return lax.all_to_all(copies, PLANE, 0, 0, tiled=True)


def dot(a, b, dims):
    return lax.dot_general(a, b, (dims, ((), ())), preferred_element_type=F32)


def ring_gather(piece):
    half = piece.shape[0] // 2
    down, up = [piece], [piece]
    for _ in range(3):
        down.append(along_z(down[-1], 1))
        up.append(along_z(up[-1], -1))
    far = jnp.concatenate([along_z(down[3][:half], 1), along_z(up[3][half:], -1)])
    return jnp.concatenate([piece, down[1], up[1], down[2], up[2], down[3], up[3], far])


SLOT = (0, 1, 3, 5, 7, 6, 4, 2)


def kernel(body, args, places, out_shape, scratch, copies, flops):
    hbm, vmem = pl.BlockSpec(memory_space=pl.ANY), pl.BlockSpec(memory_space=pltpu.VMEM)
    if not INTERPRET:
        args = [
            a
            if p == "s"
            else pltpu.with_memory_space_constraint(a, pltpu.VMEM if p == "v" else pltpu.HBM)
            for a, p in zip(args, places)
        ]
    spec_of = {"v": vmem, "h": hbm, "s": pl.BlockSpec(memory_space=pltpu.SMEM)}
    return pl.pallas_call(
        body,
        in_specs=[spec_of[p] for p in places],
        out_specs=[vmem if o.near else hbm for o in out_shape],
        out_shape=[o.placed() for o in out_shape],
        scratch_shapes=[*scratch, pltpu.SemaphoreType.DMA((copies,))],
        compiler_params=pltpu.CompilerParams(vmem_limit_bytes=26 * 2**20),
        cost_estimate=pl.CostEstimate(
            flops=flops, transcendentals=0, bytes_accessed=flops // 512
        ),
        interpret=INTERPRET,
    )(*args)


class Out:
    def __init__(self, near, shape, dtype):
        self.near, self.shape, self.dtype = near, shape, dtype

    def placed(self):
        if INTERPRET:
            return jax.ShapeDtypeStruct(self.shape, self.dtype)
        return (pltpu.VMEM if self.near else pltpu.HBM)(self.shape, self.dtype)


near = functools.partial(Out, True)
far = functools.partial(Out, False)


class Copies:
    def __init__(self, sems):
        self.sems, self.used = sems, 0

    def start(self, source, target):
        copy = pltpu.make_async_copy(source, target, self.sems.at[self.used])
        self.used += 1
        copy.start()
        return copy


def wait(copies):
    for copy in copies:
        copy.wait()


def score_body(s, part, source, *refs, scale):
    first = len(source.shape) == 4
    if first:
        queries, passages, scores, stats, sems = refs
    else:
        before, passages, scores, stats, sems = refs
        queries = source
    _, quarter, wide = part.shape
    count, full = queries.shape
    rows, width = count // 4, full // 8
    copies = Copies(sems)
    ready = []
    for d in range(4):
        for h in range(2):
            piece = part.at[jnp.where((s[0] >= d) == (h == 0), SLOT[d], SLOT[d + 4])]
            at = pl.ds(d * quarter, quarter), pl.ds(h * wide, wide)
            ready.append(copies.start(piece, passages.at[at]))
    if first:
        for x in range(4):
            for h in range(2):
                for k in range(4):
                    at = (h * 4 + k) * width
                    queries[x * rows : (x + 1) * rows, at : at + width] = source[
                        x * 4 + (s[1] + 4 - k) % 4, h
                    ]
    block = 2 * quarter
    wing = count // 2
    wait(ready)

    def chunk(k, found):
        fresh = []
        rows_at = pl.ds(pl.multiple_of(k * block, block), block)
        for j in range(2):
            at = slice(j * wing, (j + 1) * wing)
            values = dot(passages[rows_at], queries[at], ((1,), (1,))) * scale
            scores[rows_at, at] = values
            high, total = found[j]
            top = jnp.maximum(high, jnp.max(values, axis=0, keepdims=True))
            total = total * jnp.exp(high - top)
            fresh.append((top, total + jnp.sum(jnp.exp(values - top), axis=0, keepdims=True)))
        return tuple(fresh)

    def wide_row(k, j):
        return jnp.concatenate([before[4 * k + 2 * j + n : 4 * k + 2 * j + n + 1] for n in (0, 1)], 1)

    if first:
        low, none = jnp.full((1, wing), -jnp.inf, F32), jnp.zeros((1, wing), F32)
        start = ((low, none), (low, none))
    else:
        start = tuple((wide_row(0, j), wide_row(1, j)) for j in range(2))
    found = lax.fori_loop(0, 2, chunk, start)
    for x in range(4):
        j, k = divmod(x, 2)
        at = slice(k * rows, (k + 1) * rows)
        stats[x : x + 1] = found[j][0][:, at]
        stats[4 + x : 5 + x] = found[j][1][:, at]


def scored(scalars, part, source, before, count, full):
    half = 4 * part.shape[1]
    first = source.ndim == 4

    def body(*refs):
        score_body(*refs, scale=3.0 / math.sqrt(full))

    out = [near((count, full), BF16)] if first else []
    out += [
        near((half, full), BF16),
        near((half, count), F32),
        near((8, count // 4), F32),
    ]
    args = (scalars, part, source) if first else (scalars, part, source, before)
    return kernel(body, args, "shvv"[: len(args)], out, [], 8, 2 * half * count * full)


def grad_body(s, s_own, s_other, *refs):
    seen, refs = refs[:4], refs[4:]
    queries, p_own, p_other, d_own, d_other, terms, gv, bv, dv, tv, sems = refs
    half, count = s_own.shape
    full = queries.shape[1]
    block, quarter, rows, width = half // 2, half // 4, count // 4, full // 8
    logs, wanted = [], []
    for x in range(4):
        tops = [part[x : x + 1] for part in seen]
        top = functools.reduce(jnp.maximum, tops)
        total = sum(part[4 + x : 5 + x] * jnp.exp(high - top) for part, high in zip(seen, tops))
        logs.append(top + jnp.log(total))
        back = (s[10] + 4 - x) % 4
        wanted.append(sum(jnp.where(back == k, part[8:9], 0.0) for k, part in enumerate(seen)))
    log_total = jnp.concatenate(logs, axis=1)
    targets = jnp.concatenate(wanted, axis=1)

    def sent(source, b):
        target = (d_other, d_own)[source].at[pl.ds(b * block, block)]
        return pltpu.make_async_copy(dv.at[2 * source + b], target, sems.at[2 * source + b])

    def leaving(x, h, k):
        piece = terms.at[x * 4 + (s[1] + 4 - k) % 4, h]
        spot = tv.at[x, :, pl.ds((h * 4 + k) * width, width)]
        return pltpu.make_async_copy(spot, piece, sems.at[4 + 8 * x + 4 * h + k])

    for source, scores in enumerate((s_other, s_own)):

        def one(b, _):
            for k in range(2):
                base = s[2 + (1 - source) * 4 + 2 * b + k]
                ids = base + lax.broadcasted_iota(jnp.int32, (quarter, 1), 0)
                hit = (ids.astype(F32) == targets).astype(F32)
                at = pl.ds(pl.multiple_of(b * block + k * quarter, quarter), quarter)
                value = (jnp.exp(scores[at] - log_total) - hit).astype(BF16)
                bv[k * quarter : (k + 1) * quarter] = value
                at = source * half + b * block + k * quarter
                at = pl.ds(pl.multiple_of(at, quarter), quarter)
                for x in range(4):
                    gv[x, at] = value[:, x * rows : (x + 1) * rows]
            dv[2 * source + b] = dot(bv[...], queries[...], ((1,), (0,)))
            sent(source, b).start()
            return 0

        lax.fori_loop(0, 2, one, 0, unroll=True)

    def another(x, _):
        values = dot(gv[x, :half], p_other[...], ((0,), (0,)))
        values += dot(gv[x, half:], p_own[...], ((0,), (0,)))
        tv[x] = values.astype(BF16)
        for h in range(2):
            for k in range(4):
                leaving(x, h, k).start()
        return 0

    lax.fori_loop(0, 4, another, 0)
    for source in range(2):
        for b in range(2):
            sent(source, b).wait()
    for x in range(4):
        for h in range(2):
            for k in range(4):
                leaving(x, h, k).wait()


def gradients(scalars, s_own, s_other, seen, queries, p_own, p_other):
    half, count = s_own.shape
    full = queries.shape[1]
    out = [
        far((half, full), F32),
        far((half, full), F32),
        far((16, 2, count // 4, full // 8), BF16),
    ]
    scratch = [
        pltpu.VMEM((4, 2 * half, count // 4), BF16),
        pltpu.VMEM((half // 2, count), BF16),
        pltpu.VMEM((4, half // 2, full), F32),
        pltpu.VMEM((4, count // 4, full), BF16),
    ]
    args = (scalars, s_own, s_other, *seen, queries, p_own, p_other)
    return kernel(grad_body, args, "s" + 9 * "v", out, scratch, 40, 8 * half * count * full)


def combine_body(s, own, theirs, *refs):
    outs, (av, bv, fv, ov, sems) = refs[:9], refs[9:]
    quarter, wide = outs[0].shape
    half = quarter // 2
    copies = Copies(sems)
    order = (3, 0, 2, 1)
    loads = {}
    for d in order:
        at = pl.ds(d * quarter, quarter)
        loads[d] = (
            copies.start(own.at[at], av.at[at]),
            copies.start(theirs.at[at], bv.at[at]),
        )
    ends = []
    for d in order:
        wait(loads[d])
        at = slice(d * quarter, (d + 1) * quarter)
        pair = av[at] + bv[at]
        left, right = pair[:, :wide], pair[:, wide:]
        here = s[0] >= d
        for k, value in ((d, jnp.where(here, left, right)), (d + 4, jnp.where(here, right, left))):
            if k in (0, 1, 7):
                place = (0, 1, 7).index(k)
                fv[place] = value
                ends.append(copies.start(fv.at[place], outs[place]))
                continue
            ov[k - 2] = value.astype(BF16)
            if k == 4:
                ends.append(copies.start(ov.at[2, pl.ds(0, half)], outs[7]))
                ends.append(copies.start(ov.at[2, pl.ds(half, half)], outs[8]))
            else:
                ends.append(copies.start(ov.at[k - 2], outs[3 + (2, 3, 5, 6).index(k)]))
    wait(ends)


def combined(scalars, own, theirs):
    rows, full = own.shape
    quarter, wide = rows // 4, full // 2
    scratch = [
        pltpu.VMEM((rows, full), F32),
        pltpu.VMEM((rows, full), F32),
        pltpu.VMEM((3, quarter, wide), F32),
        pltpu.VMEM((5, quarter, wide), BF16),
    ]
    out = [far((quarter, wide), F32)] * 3 + [far((quarter, wide), BF16)] * 4
    out += [far((quarter // 2, wide), BF16)] * 2
    return kernel(combine_body, (scalars, own, theirs), "shh", out, scratch, 17, 2**31)


def local(queries, passages, positive):
    return step(queries, passages, positive)


def step(queries, passages, positive):
    rows, width = queries.shape
    half, quarter = rows // 2, rows // 4
    full, count = 8 * width, 2 * rows
    x, y, c = (lax.axis_index(a) for a in ("x", "y", "c"))
    zl, zh = lax.axis_index("zl"), lax.axis_index("zh")

    kept = lax.dynamic_slice(queries, (zh * half, 0), (half, width))
    sent = lax.dynamic_slice(queries, ((1 - zh) * half, 0), (half, width))
    copies = jnp.stack([kept, swapped(sent, "zh")])
    pieces = to_plane(copies)

    mine = [
        lax.dynamic_slice(passages, ((y + d) % 4 * quarter, 0), (quarter, width)) for d in range(4)
    ]
    crossed = [along(mine[d], "y", d) for d in (1, 2, 3)]
    passage_part = jnp.concatenate([mine[0], *crossed], axis=1)
    own = ring_gather(passage_part).reshape(8, quarter, 4 * width)
    other = swapped(own, "c")

    source_c = jnp.stack([c, 1 - c])
    group = (((zl - jnp.arange(4)) % 4) * 4 + x)[None, :] * 2 + source_c[:, None]
    first = (group * rows + y * quarter).reshape(8)
    scalars = jnp.concatenate([zl[None], y[None], first, x[None]]).astype(jnp.int32)

    block_queries, p_own, s_own, half_stats = scored(scalars, own, pieces, None, count, full)
    p_other, s_other, stats = scored(scalars, other, block_queries, half_stats, count, full)
    wanted = lax.dynamic_slice(positive, (zh * half,), (half,)).astype(F32)
    seen = [stats] + [along(stats, "y", d) for d in (1, 2, 3)]
    tops = functools.reduce(jnp.maximum, [part[:4] for part in seen])
    totals = sum(part[4:] * jnp.exp(part[:4] - tops) for part in seen)
    stats = jnp.concatenate([tops, totals, wanted[None]])
    seen = [stats] + [along(stats, "x", d) for d in (1, 2, 3)]

    d_own, d_other, terms = gradients(
        scalars, s_own, s_other, seen, block_queries, p_own, p_other
    )
    theirs = swapped(d_other, "c")
    terms = lax.all_to_all(terms, PLANE, 0, 0, tiled=True)
    mine, down, up, d2, d3, d5, d6, low, high = combined(scalars, d_own, theirs)
    low, high = along_z(low, -3), along_z(high, 3)
    d3, d5 = along_z(d3, -2), along_z(d5, 2)
    d2, d6 = along_z(d2, -2), along_z(d6, 2)
    rest, rest_up = ((0, quarter // 2), (0, 0)), ((quarter // 2, 0), (0, 0))
    down = (down + d3.astype(F32) + jnp.pad(low.astype(F32), rest)).astype(BF16)
    up = (up + d5.astype(F32) + jnp.pad(high.astype(F32), rest_up)).astype(BF16)
    down, up = along_z(down, -1), along_z(up, 1)
    total = mine
    for part in (d2, d6, down, up):
        total += part.astype(F32)
    total = total.astype(BF16)
    slices = [total[:, k * width : (k + 1) * width] for k in range(4)]
    slices = [slices[0]] + [along(slices[k], "y", -k) for k in (1, 2, 3)]
    grad_passages = jnp.concatenate(
        [lax.select_n((q + 4 - y) % 4, *slices) for q in range(4)]
    )

    grad_queries = jnp.sum(terms.astype(F32), axis=0).astype(BF16)
    kept, received = grad_queries[0], swapped(grad_queries[1], "zh")
    grad_queries = jnp.where(
        zh == 0, jnp.concatenate([kept, received]), jnp.concatenate([received, kept])
    )
    return grad_queries, grad_passages


def solution(mesh):
    finer = Mesh(mesh.devices.reshape(4, 4, 2, 2, 4), ("zl", "x", "c", "zh", "y"))
    groups = ("zl", "x", "c")
    return jax.shard_map(
        step if INTERPRET else local,
        mesh=finer,
        in_specs=(P(groups, WIDTH), P(groups, WIDTH), P(groups)),
        out_specs=(P(groups, WIDTH), P(groups, WIDTH)),
        check_vma=False,
    )
```

profile of v0, /device:TPU:68, one launch (start us, length us, event | category | flops | bytes accessed | tf_op | source)
XLA Modules:
  0.0 233.1 jit_solution(1624870731937601916)
XLA Ops:
  0.6 1.0 dynamic-slice_bitcast_fusion
  1.6 5.5 %collective-permute-start.11 = (bf16[384,128]{1,0:T(8,128)(2,1)S(1)}, bf16[384,128]{1,0:T(8,128)(2,1)S(1)}, u32[]{:S(2)}, u32[]{:S(2)}) collective-permute-start(bf16[384,128]{1,0:T(8,128)(2,1)S(1)} %get-tuple-element.52), channel_id=1, source_target_pairs={{0,4},{4,0},{1,5},{5,1},{2,6},{6,2},{3,7},{7,3},{8,12},{12,8},{9,1... | collective-permute-start | bytes 294920 | tf_op jit(solution)/shard_map/ppermute | solution.py:28
  7.1 5.3 %collective-permute-done.11 = bf16[384,128]{1,0:T(8,128)(2,1)S(1)} collective-permute-done((bf16[384,128]{1,0:T(8,128)(2,1)S(1)}, bf16[384,128]{1,0:T(8,128)(2,1)S(1)}, u32[]{:S(2)}, u32[]{:S(2)}) %collective-permute-start.11) | collective-permute-done | bytes 98336 | tf_op jit(solution)/shard_map/ppermute | solution.py:28
  12.4 2.4 %broadcast_in_dim.23 = bf16[16,2,384,128]{3,2,1,0:T(8,128)(2,1)} broadcast(bf16[2,384,128]{2,1,0:T(8,128)(2,1)S(1)} %pad_maximum_fusion.1), dimensions={1,2,3} | broadcast | bytes 3342336 | tf_op jit(solution)/shard_map/broadcast_in_dim | solution.py:32
  14.7 7.6 %all-to-all-start = ((bf16[16,2,384,128]{3,2,1,0:T(8,128)(2,1)}), bf16[16,2,384,128]{3,2,1,0:T(8,128)(2,1)S(1)}, u32[]{:S(2)}, u32[]{:S(2)}) async-start(bf16[16,2,384,128]{3,2,1,0:T(8,128)(2,1)} %broadcast_in_dim.23), calls=%async_computation | async-start | bytes 6291456 | tf_op jit(solution)/shard_map/all_to_all | solution.py:33
  22.3 1.5 collective-permute-start
  23.9 2.7 %collective-permute-start.1 = (bf16[192,128]{1,0:T(8,128)(2,1)S(1)}, bf16[192,128]{1,0:T(8,128)(2,1)S(1)}, u32[]{:S(2)}, u32[]{:S(2)}) collective-permute-start(bf16[192,128]{1,0:T(8,128)(2,1)S(1)} %get-tuple-element.58), channel_id=1, source_target_pairs={{0,2},{1,3},{2,0},{3,1},{4,6},{5,7},{6,4},{7,5},{8,10},{9,11},{10,... | collective-permute-start | bytes 147464 | tf_op jit(solution)/shard_map/ppermute | solution.py:24
  26.6 1.5 collective-permute-start.2
  28.0 30.8 %collective-permute-done = bf16[192,128]{1,0:T(8,128)(2,1)S(1)} collective-permute-done((bf16[192,128]{1,0:T(8,128)(2,1)S(1)}, bf16[192,128]{1,0:T(8,128)(2,1)S(1)}, u32[]{:S(2)}, u32[]{:S(2)}) %collective-permute-start) | collective-permute-done | bytes 49184 | tf_op jit(solution)/shard_map/ppermute | solution.py:24
  60.1 1.6 collective-permute-start.3
  62.1 3.6 %collective-permute-done.3 = bf16[192,512]{1,0:T(8,128)(2,1)S(1)} collective-permute-done((bf16[192,512]{1,0:T(8,128)(2,1)S(1)}, bf16[192,512]{1,0:T(8,128)(2,1)S(1)}, u32[]{:S(2)}, u32[]{:S(2)}) %collective-permute-start.3) | collective-permute-done | bytes 196640 | tf_op jit(solution)/shard_map/ppermute | solution.py:20
  65.7 2.5 %collective-permute-start.5 = (bf16[192,512]{1,0:T(8,128)(2,1)S(1)}, bf16[192,512]{1,0:T(8,128)(2,1)S(1)}, u32[]{:S(2)}, u32[]{:S(2)}) collective-permute-start(bf16[192,512]{1,0:T(8,128)(2,1)S(1)} %collective-permute-done.3), channel_id=1, source_target_pairs={{0,64},{64,128},{128,192},{192,4},{4,68},{68,132},{132,196},{196,0... | collective-permute-start | bytes 589832 | tf_op jit(solution)/shard_map/ppermute | solution.py:20
  70.1 2.0 collective-permute-done.5
  72.1 4.0 %collective-permute-start.7 = (bf16[192,512]{1,0:T(8,128)(2,1)S(1)}, bf16[192,512]{1,0:T(8,128)(2,1)S(1)}, u32[]{:S(2)}, u32[]{:S(2)}) collective-permute-start(bf16[192,512]{1,0:T(8,128)(2,1)S(1)} %collective-permute-done.5), channel_id=1, source_target_pairs={{0,64},{64,128},{128,192},{192,4},{4,68},{68,132},{132,196},{196,0... | collective-permute-start | bytes 589832 | tf_op jit(solution)/shard_map/ppermute | solution.py:20
  78.0 2.3 collective-permute-done.7
  80.3 3.7 %collective-permute-start.9 = (bf16[96,512]{1,0:T(8,128)(2,1)S(1)}, bf16[96,512]{1,0:T(8,128)(2,1)S(1)}, u32[]{:S(2)}, u32[]{:S(2)}) collective-permute-start(bf16[96,512]{1,0:T(8,128)(2,1)S(1)} %slice.68), channel_id=1, source_target_pairs={{0,64},{64,128},{128,192},{192,4},{4,68},{68,132},{132,196},{196,0... | collective-permute-start | bytes 294920 | tf_op jit(solution)/shard_map/ppermute | solution.py:20
  84.0 0.8 collective-permute-done.8
  87.0 3.6 %collective-permute-done.10 = bf16[96,512]{1,0:T(8,128)(2,1)S(1)} collective-permute-done((bf16[96,512]{1,0:T(8,128)(2,1)S(1)}, bf16[96,512]{1,0:T(8,128)(2,1)S(1)}, u32[]{:S(2)}, u32[]{:S(2)}) %collective-permute-start.10) | collective-permute-done | bytes 98336 | tf_op jit(solution)/shard_map/ppermute | solution.py:20
  91.5 5.6 %shard_map.50 = (bf16[1536,1024]{1,0:T(8,128)(2,1)S(1)}, bf16[768,1024]{1,0:T(8,128)(2,1)S(1)}, f32[768,1536]{1,0:T(8,128)S(1)}, f32[8,384]{1,0:T(8,128)S(1)}) custom-call(s32[11]{0:T(128)S(1)} %pad_add_fusion.1.refs_0_.s, bf16[8,192,512]{2,1,0:T(8,128)(2,1)} %bitcast.5.refs_1_, bf16[16,2,384,128]{3,2,1,0:T(8,128)(2,1)S(1)} %all-to-all-done.refs_2_), custom_call_target="tpu_custom_call" | custom-call | flops 2415919104 | bytes 4718592 | tf_op jit(solution)/shard_map/pallas_call | solution.py:63
  97.2 5.6 %shard_map.51 = (bf16[768,1024]{1,0:T(8,128)(2,1)S(1)}, f32[768,1536]{1,0:T(8,128)S(1)}, f32[8,384]{1,0:T(8,128)S(1)}) custom-call(s32[11]{0:T(128)S(1)} %pad_add_fusion.1.refs_0_.s, bf16[8,192,512]{2,1,0:T(8,128)(2,1)} %collective-permute-done.12.refs_1_, bf16[1536,1024]{1,0:T(8,128)(2,1)S(1)} %get-tuple-element.22.refs_2_.refs_4_, ...), custom_call_target="tpu_custom_call" | custom-call | flops 2415919104 | bytes 4718592 | tf_op jit(solution)/shard_map/pallas_call | solution.py:63
  103.2 5.0 %collective-permute-start.14 = (f32[8,384]{1,0:T(8,128)S(1)}, f32[8,384]{1,0:T(8,128)S(1)}, u32[]{:S(2)}, u32[]{:S(2)}) collective-permute-start(f32[8,384]{1,0:T(8,128)S(1)} %get-tuple-element.25), channel_id=1, source_target_pairs={{0,2},{1,3},{2,0},{3,1},{4,6},{5,7},{6,4},{7,5},{8,10},{9,11},{10,... | collective-permute-start | bytes 36872 | tf_op jit(solution)/shard_map/ppermute | solution.py:24
  108.2 2.5 %collective-permute-start.15 = (f32[8,384]{1,0:T(8,128)S(1)}, f32[8,384]{1,0:T(8,128)S(1)}, u32[]{:S(2)}, u32[]{:S(2)}) collective-permute-start(f32[8,384]{1,0:T(8,128)S(1)} %get-tuple-element.25), channel_id=1, source_target_pairs={{0,3},{1,0},{2,1},{3,2},{4,7},{5,4},{6,5},{7,6},{8,11},{9,8},{10,9... | collective-permute-start | bytes 36872 | tf_op jit(solution)/shard_map/ppermute | solution.py:24
  110.9 1.3 collective-permute-done.15
  112.3 1.6 collective-permute-start.17
  113.9 1.2 collective-permute-start.18
  115.1 1.1 collective-permute-done.16.refs_1_
  116.2 1.5 collective-permute-done.17.refs_2_
  117.7 0.7 collective-permute-done.18.refs_3_
  118.4 12.7 %shard_map.52 = (f32[768,1024]{1,0:T(8,128)}, f32[768,1024]{1,0:T(8,128)}, bf16[16,2,384,128]{3,2,1,0:T(8,128)(2,1)}) custom-call(s32[11]{0:T(128)S(1)} %pad_add_fusion.1.refs_0_.s, f32[768,1536]{1,0:T(8,128)S(1)} %get-tuple-element.21.s_own, f32[768,1536]{1,0:T(8,128)S(1)} %get-tuple-element.24.s_other, f32[9,384]{1,0:T(8,128)S(1)} %pad_maximum_fusion.3.refs_0_, ...), custom_call_target="tpu_custom_call" | custom-call | flops 9663676416 | bytes 18874368 | tf_op jit(solution)/shard_map/pallas_call | solution.py:63
  131.2 9.3 %all-to-all-start.1 = ((bf16[16,2,384,128]{3,2,1,0:T(8,128)(2,1)}), bf16[16,2,384,128]{3,2,1,0:T(8,128)(2,1)S(1)}, u32[]{:S(2)}, u32[]{:S(2)}) async-start(bf16[16,2,384,128]{3,2,1,0:T(8,128)(2,1)} %get-tuple-element.28), calls=%async_computation.1 | async-start | bytes 6291456 | tf_op jit(solution)/shard_map/all_to_all | solution.py:356
  140.5 4.8 %shard_map.53 = (f32[192,512]{1,0:T(8,128)}, f32[192,512]{1,0:T(8,128)}, f32[192,512]{1,0:T(8,128)}, bf16[192,512]{1,0:T(8,128)(2,1)}, bf16[192,512]{1,0:T(8,128...) custom-call(s32[11]{0:T(128)S(1)} %pad_add_fusion.1.refs_0_.s, ...), custom_call_target="tpu_custom_call" | custom-call | flops 2147483648 | bytes 4194304 | tf_op jit(solution)/shard_map/pallas_call | solution.py:63
  145.7 2.6 %collective-permute-start.24 = (bf16[96,512]{1,0:T(8,128)(2,1)}, bf16[96,512]{1,0:T(8,128)(2,1)}, u32[]{:S(2)}, u32[]{:S(2)}) collective-permute-start(bf16[96,512]{1,0:T(8,128)(2,1)} %get-tuple-element.36), channel_id=1, source_target_pairs={{0,68},{64,132},{128,196},{192,0},{4,64},{68,128},{132,192},{196,4... | collective-permute-start | bytes 294920 | tf_op jit(solution)/shard_map/ppermute | solution.py:20
  148.3 36.6 %all-to-all-done.1 = bf16[16,2,384,128]{3,2,1,0:T(8,128)(2,1)S(1)} async-done(((bf16[16,2,384,128]{3,2,1,0:T(8,128)(2,1)}), bf16[16,2,384,128]{3,2,1,0:T(8,128)(2,1)S(1)}, u32[]{:S(2)}, u32[]{:S(2)}) %all-to-all-start.1) | async-done | bytes 3145760 | tf_op jit(solution)/shard_map/all_to_all | solution.py:356
  185.4 3.3 %collective-permute-start.26 = (bf16[192,512]{1,0:T(8,128)(2,1)}, bf16[192,512]{1,0:T(8,128)(2,1)S(1)}, u32[]{:S(2)}, u32[]{:S(2)}) collective-permute-start(bf16[192,512]{1,0:T(8,128)(2,1)} %get-tuple-element.38), channel_id=1, source_target_pairs={{0,128},{64,192},{128,4},{192,68},{4,132},{68,196},{132,0},{196,64... | collective-permute-start | bytes 589832 | tf_op jit(solution)/shard_map/ppermute | solution.py:20
  189.3 1.9 collective-permute-start.21
  191.2 2.3 collective-permute-start.22
  193.4 1.1 add_convert_fusion.2
  194.5 1.2 collective-permute-start.25
  195.7 9.7 %collective-permute-done.27 = bf16[96,512]{1,0:T(8,128)(2,1)S(1)} collective-permute-done((bf16[96,512]{1,0:T(8,128)(2,1)}, bf16[96,512]{1,0:T(8,128)(2,1)S(1)}, u32[]{:S(2)}, u32[]{:S(2)}) %collective-permute-start.27) | collective-permute-done | bytes 98336 | tf_op jit(solution)/shard_map/ppermute | solution.py:20
  205.4 1.1 add_convert_fusion.1
  206.8 3.6 %collective-permute-start.19 = (bf16[384,128]{1,0:T(8,128)(2,1)S(1)}, bf16[384,128]{1,0:T(8,128)(2,1)S(1)}, u32[]{:S(2)}, u32[]{:S(2)}) collective-permute-start(bf16[384,128]{1,0:T(8,128)(2,1)S(1)} %get-tuple-element.50), channel_id=1, source_target_pairs={{0,4},{4,0},{1,5},{5,1},{2,6},{6,2},{3,7},{7,3},{8,12},{12,8},{9,1... | collective-permute-start | bytes 294920 | tf_op jit(solution)/shard_map/ppermute | solution.py:28
  210.4 2.2 collective-permute-done.22
  212.6 7.8 %collective-permute-done.28 = bf16[192,512]{1,0:T(8,128)(2,1)S(1)} collective-permute-done((bf16[192,512]{1,0:T(8,128)(2,1)S(1)}, bf16[192,512]{1,0:T(8,128)(2,1)S(1)}, u32[]{:S(2)}, u32[]{:S(2)}) %collective-permute-start.28) | collective-permute-done | bytes 196640 | tf_op jit(solution)/shard_map/ppermute | solution.py:20
  220.6 5.5 %collective-permute-start.29 = (bf16[192,128]{1,0:T(8,128)(2,1)S(1)}, bf16[192,128]{1,0:T(8,128)(2,1)S(1)}, u32[]{:S(2)}, u32[]{:S(2)}) collective-permute-start(bf16[192,128]{1,0:T(8,128)(2,1)S(1)} %get-tuple-element.46), channel_id=1, source_target_pairs={{0,3},{1,0},{2,1},{3,2},{4,7},{5,4},{6,5},{7,6},{8,11},{9,8},{10,9... | collective-permute-start | bytes 147464 | tf_op jit(solution)/shard_map/ppermute | solution.py:24
  226.1 0.9 collective-permute-start.30
  227.0 1.3 collective-permute-start.31
  228.4 0.7 maximum_select_fusion
  229.1 2.6 %collective-permute-done.30 = bf16[192,128]{1,0:T(8,128)(2,1)S(1)} collective-permute-done((bf16[192,128]{1,0:T(8,128)(2,1)S(1)}, bf16[192,128]{1,0:T(8,128)(2,1)S(1)}, u32[]{:S(2)}, u32[]{:S(2)}) %collective-permute-start.30) | collective-permute-done | bytes 49184 | tf_op jit(solution)/shard_map/ppermute | solution.py:24
  (63 shorter events, 12.7 us)
Async XLA Ops:
  1.6 10.7 %collective-permute-start.11 = (bf16[384,128]{1,0:T(8,128)(2,1)S(1)}, bf16[384,128]{1,0:T(8,128)(2,1)S(1)}, u32[]{:S(2)}, u32[]{:S(2)}) collective-permute-start(bf16[384,128]{1,0:T(8,128)(2,1)S(1)} %get-tuple-element.52), channel_id=1, source_target_pairs={{0,4},{4,0},{1,5},{5,1},{2,6},{6,2},{3,7},{7,3},{8,12},{12,8},{9,1... | collective-permute-start | bytes 294920 | tf_op jit(solution)/shard_map/ppermute | solution.py:28
  14.7 7.6 %copy-start.1 = (bf16[768,128]{1,0:T(8,128)(2,1)S(1)}, bf16[768,128]{1,0:T(8,128)(2,1)}, u32[]{:S(2)}) copy-start(bf16[768,128]{1,0:T(8,128)(2,1)} %param.4) | copy-start | bytes 589828
  14.7 76.8 %all-to-all-start = ((bf16[16,2,384,128]{3,2,1,0:T(8,128)(2,1)}), bf16[16,2,384,128]{3,2,1,0:T(8,128)(2,1)S(1)}, u32[]{:S(2)}, u32[]{:S(2)}) async-start(bf16[16,2,384,128]{3,2,1,0:T(8,128)(2,1)} %broadcast_in_dim.23), calls=%async_computation | async-start | bytes 6291456 | tf_op jit(solution)/shard_map/all_to_all | solution.py:33
  22.3 36.4 %collective-permute-start = (bf16[192,128]{1,0:T(8,128)(2,1)S(1)}, bf16[192,128]{1,0:T(8,128)(2,1)S(1)}, u32[]{:S(2)}, u32[]{:S(2)}) collective-permute-start(bf16[192,128]{1,0:T(8,128)(2,1)S(1)} %get-tuple-element.56), channel_id=1, source_target_pairs={{0,1},{1,2},{2,3},{3,0},{4,5},{5,6},{6,7},{7,4},{8,9},{9,10},{10,1... | collective-permute-start | bytes 147464 | tf_op jit(solution)/shard_map/ppermute | solution.py:24
  23.9 34.9 %collective-permute-start.1 = (bf16[192,128]{1,0:T(8,128)(2,1)S(1)}, bf16[192,128]{1,0:T(8,128)(2,1)S(1)}, u32[]{:S(2)}, u32[]{:S(2)}) collective-permute-start(bf16[192,128]{1,0:T(8,128)(2,1)S(1)} %get-tuple-element.58), channel_id=1, source_target_pairs={{0,2},{1,3},{2,0},{3,1},{4,6},{5,7},{6,4},{7,5},{8,10},{9,11},{10,... | collective-permute-start | bytes 147464 | tf_op jit(solution)/shard_map/ppermute | solution.py:24
  26.6 32.8 %collective-permute-start.2 = (bf16[192,128]{1,0:T(8,128)(2,1)S(1)}, bf16[192,128]{1,0:T(8,128)(2,1)S(1)}, u32[]{:S(2)}, u32[]{:S(2)}) collective-permute-start(bf16[192,128]{1,0:T(8,128)(2,1)S(1)} %get-tuple-element.57), channel_id=1, source_target_pairs={{0,3},{1,0},{2,1},{3,2},{4,7},{5,4},{6,5},{7,6},{8,11},{9,8},{10,9... | collective-permute-start | bytes 147464 | tf_op jit(solution)/shard_map/ppermute | solution.py:24
  60.1 5.7 %collective-permute-start.3 = (bf16[192,512]{1,0:T(8,128)(2,1)S(1)}, bf16[192,512]{1,0:T(8,128)(2,1)S(1)}, u32[]{:S(2)}, u32[]{:S(2)}) collective-permute-start(bf16[192,512]{1,0:T(8,128)(2,1)S(1)} %get-tuple-element.53), channel_id=1, source_target_pairs={{0,64},{64,128},{128,192},{192,4},{4,68},{68,132},{132,196},{196,0... | collective-permute-start | bytes 589832 | tf_op jit(solution)/shard_map/ppermute | solution.py:20
  61.7 7.0 %collective-permute-start.4 = (bf16[192,512]{1,0:T(8,128)(2,1)S(1)}, bf16[192,512]{1,0:T(8,128)(2,1)S(1)}, u32[]{:S(2)}, u32[]{:S(2)}) collective-permute-start(bf16[192,512]{1,0:T(8,128)(2,1)S(1)} %get-tuple-element.53), channel_id=1, source_target_pairs={{0,196},{64,0},{128,64},{192,128},{4,192},{68,4},{132,68},{196,132... | collective-permute-start | bytes 589832 | tf_op jit(solution)/shard_map/ppermute | solution.py:20
  65.7 6.4 %collective-permute-start.5 = (bf16[192,512]{1,0:T(8,128)(2,1)S(1)}, bf16[192,512]{1,0:T(8,128)(2,1)S(1)}, u32[]{:S(2)}, u32[]{:S(2)}) collective-permute-start(bf16[192,512]{1,0:T(8,128)(2,1)S(1)} %collective-permute-done.3), channel_id=1, source_target_pairs={{0,64},{64,128},{128,192},{192,4},{4,68},{68,132},{132,196},{196,0... | collective-permute-start | bytes 589832 | tf_op jit(solution)/shard_map/ppermute | solution.py:20
  68.7 7.9 %collective-permute-start.6 = (bf16[192,512]{1,0:T(8,128)(2,1)S(1)}, bf16[192,512]{1,0:T(8,128)(2,1)S(1)}, u32[]{:S(2)}, u32[]{:S(2)}) collective-permute-start(bf16[192,512]{1,0:T(8,128)(2,1)S(1)} %collective-permute-done.4), channel_id=1, source_target_pairs={{0,196},{64,0},{128,64},{192,128},{4,192},{68,4},{132,68},{196,132... | collective-permute-start | bytes 589832 | tf_op jit(solution)/shard_map/ppermute | solution.py:20
  72.1 8.2 %collective-permute-start.7 = (bf16[192,512]{1,0:T(8,128)(2,1)S(1)}, bf16[192,512]{1,0:T(8,128)(2,1)S(1)}, u32[]{:S(2)}, u32[]{:S(2)}) collective-permute-start(bf16[192,512]{1,0:T(8,128)(2,1)S(1)} %collective-permute-done.5), channel_id=1, source_target_pairs={{0,64},{64,128},{128,192},{192,4},{4,68},{68,132},{132,196},{196,0... | collective-permute-start | bytes 589832 | tf_op jit(solution)/shard_map/ppermute | solution.py:20
  76.6 8.2 %collective-permute-start.8 = (bf16[192,512]{1,0:T(8,128)(2,1)S(1)}, bf16[192,512]{1,0:T(8,128)(2,1)S(1)}, u32[]{:S(2)}, u32[]{:S(2)}) collective-permute-start(bf16[192,512]{1,0:T(8,128)(2,1)S(1)} %collective-permute-done.6), channel_id=1, source_target_pairs={{0,196},{64,0},{128,64},{192,128},{4,192},{68,4},{132,68},{196,132... | collective-permute-start | bytes 589832 | tf_op jit(solution)/shard_map/ppermute | solution.py:20
  80.3 6.0 %collective-permute-start.9 = (bf16[96,512]{1,0:T(8,128)(2,1)S(1)}, bf16[96,512]{1,0:T(8,128)(2,1)S(1)}, u32[]{:S(2)}, u32[]{:S(2)}) collective-permute-start(bf16[96,512]{1,0:T(8,128)(2,1)S(1)} %slice.68), channel_id=1, source_target_pairs={{0,64},{64,128},{128,192},{192,4},{4,68},{68,132},{132,196},{196,0... | collective-permute-start | bytes 294920 | tf_op jit(solution)/shard_map/ppermute | solution.py:20
  84.9 5.7 %collective-permute-start.10 = (bf16[96,512]{1,0:T(8,128)(2,1)S(1)}, bf16[96,512]{1,0:T(8,128)(2,1)S(1)}, u32[]{:S(2)}, u32[]{:S(2)}) collective-permute-start(bf16[96,512]{1,0:T(8,128)(2,1)S(1)} %slice.69), channel_id=1, source_target_pairs={{0,196},{64,0},{128,64},{192,128},{4,192},{68,4},{132,68},{196,132... | collective-permute-start | bytes 294920 | tf_op jit(solution)/shard_map/ppermute | solution.py:20
  91.2 5.9 %collective-permute-start.12 = (bf16[8,192,512]{2,1,0:T(8,128)(2,1)}, bf16[8,192,512]{2,1,0:T(8,128)(2,1)}, u32[]{:S(2)}, u32[]{:S(2)}) collective-permute-start(bf16[8,192,512]{2,1,0:T(8,128)(2,1)} %bitcast.5.refs_1_), channel_id=1, source_target_pairs={{0,8},{8,0},{1,9},{9,1},{2,10},{10,2},{3,11},{11,3},{4,12},{12,4},... | collective-permute-start | bytes 4718600 | tf_op jit(solution)/shard_map/ppermute | solution.py:28
  97.2 13.6 %copy-start.2 = (s32[768]{0:T(1024)S(1)}, s32[768]{0:T(1024)}, u32[]{:S(2)}) copy-start(s32[768]{0:T(1024)} %param.5) | copy-start | bytes 9220
  102.8 8.1 %collective-permute-start.13 = (f32[8,384]{1,0:T(8,128)S(1)}, f32[8,384]{1,0:T(8,128)S(1)}, u32[]{:S(2)}, u32[]{:S(2)}) collective-permute-start(f32[8,384]{1,0:T(8,128)S(1)} %get-tuple-element.25), channel_id=1, source_target_pairs={{0,1},{1,2},{2,3},{3,0},{4,5},{5,6},{6,7},{7,4},{8,9},{9,10},{10,1... | collective-permute-start | bytes 36872 | tf_op jit(solution)/shard_map/ppermute | solution.py:24
  103.2 7.6 %collective-permute-start.14 = (f32[8,384]{1,0:T(8,128)S(1)}, f32[8,384]{1,0:T(8,128)S(1)}, u32[]{:S(2)}, u32[]{:S(2)}) collective-permute-start(f32[8,384]{1,0:T(8,128)S(1)} %get-tuple-element.25), channel_id=1, source_target_pairs={{0,2},{1,3},{2,0},{3,1},{4,6},{5,7},{6,4},{7,5},{8,10},{9,11},{10,... | collective-permute-start | bytes 36872 | tf_op jit(solution)/shard_map/ppermute | solution.py:24
  108.2 3.9 %collective-permute-start.15 = (f32[8,384]{1,0:T(8,128)S(1)}, f32[8,384]{1,0:T(8,128)S(1)}, u32[]{:S(2)}, u32[]{:S(2)}) collective-permute-start(f32[8,384]{1,0:T(8,128)S(1)} %get-tuple-element.25), channel_id=1, source_target_pairs={{0,3},{1,0},{2,1},{3,2},{4,7},{5,4},{6,5},{7,6},{8,11},{9,8},{10,9... | collective-permute-start | bytes 36872 | tf_op jit(solution)/shard_map/ppermute | solution.py:24
  112.2 4.0 %collective-permute-start.16 = (f32[9,384]{1,0:T(8,128)S(1)}, f32[9,384]{1,0:T(8,128)S(1)}, u32[]{:S(2)}, u32[]{:S(2)}) collective-permute-start(f32[9,384]{1,0:T(8,128)S(1)} %pad_maximum_fusion.3.refs_0_), channel_id=1, source_target_pairs={{0,16},{16,32},{32,48},{48,0},{1,17},{17,33},{33,49},{49,1},{2,18}... | collective-permute-start | bytes 41480 | tf_op jit(solution)/shard_map/ppermute | solution.py:24
  112.3 5.4 %collective-permute-start.17 = (f32[9,384]{1,0:T(8,128)S(1)}, f32[9,384]{1,0:T(8,128)S(1)}, u32[]{:S(2)}, u32[]{:S(2)}) collective-permute-start(f32[9,384]{1,0:T(8,128)S(1)} %pad_maximum_fusion.3.refs_0_), channel_id=1, source_target_pairs={{0,32},{16,48},{32,0},{48,16},{1,33},{17,49},{33,1},{49,17},{2,34}... | collective-permute-start | bytes 41480 | tf_op jit(solution)/shard_map/ppermute | solution.py:24
  113.9 4.6 %collective-permute-start.18 = (f32[9,384]{1,0:T(8,128)S(1)}, f32[9,384]{1,0:T(8,128)S(1)}, u32[]{:S(2)}, u32[]{:S(2)}) collective-permute-start(f32[9,384]{1,0:T(8,128)S(1)} %pad_maximum_fusion.3.refs_0_), channel_id=1, source_target_pairs={{0,48},{16,0},{32,16},{48,32},{1,49},{17,1},{33,17},{49,33},{2,50}... | collective-permute-start | bytes 41480 | tf_op jit(solution)/shard_map/ppermute | solution.py:24
  131.1 9.4 %collective-permute-start.20 = (f32[768,1024]{1,0:T(8,128)}, f32[768,1024]{1,0:T(8,128)}, u32[]{:S(2)}, u32[]{:S(2)}) collective-permute-start(f32[768,1024]{1,0:T(8,128)} %get-tuple-element.30), channel_id=1, source_target_pairs={{0,8},{8,0},{1,9},{9,1},{2,10},{10,2},{3,11},{11,3},{4,12},{12,4},... | collective-permute-start | bytes 9437192 | tf_op jit(solution)/shard_map/ppermute | solution.py:28
  131.2 53.7 %all-to-all-start.1 = ((bf16[16,2,384,128]{3,2,1,0:T(8,128)(2,1)}), bf16[16,2,384,128]{3,2,1,0:T(8,128)(2,1)S(1)}, u32[]{:S(2)}, u32[]{:S(2)}) async-start(bf16[16,2,384,128]{3,2,1,0:T(8,128)(2,1)} %get-tuple-element.28), calls=%async_computation.1 | async-start | bytes 6291456 | tf_op jit(solution)/shard_map/all_to_all | solution.py:356
  145.3 48.1 %collective-permute-start.23 = (bf16[192,512]{1,0:T(8,128)(2,1)}, bf16[192,512]{1,0:T(8,128)(2,1)S(1)}, u32[]{:S(2)}, u32[]{:S(2)}) collective-permute-start(bf16[192,512]{1,0:T(8,128)(2,1)} %get-tuple-element.35), channel_id=1, source_target_pairs={{0,132},{64,196},{128,0},{192,64},{4,128},{68,192},{132,4},{196,68... | collective-permute-start | bytes 589832 | tf_op jit(solution)/shard_map/ppermute | solution.py:20
  145.7 45.5 %collective-permute-start.24 = (bf16[96,512]{1,0:T(8,128)(2,1)}, bf16[96,512]{1,0:T(8,128)(2,1)}, u32[]{:S(2)}, u32[]{:S(2)}) collective-permute-start(bf16[96,512]{1,0:T(8,128)(2,1)} %get-tuple-element.36), channel_id=1, source_target_pairs={{0,68},{64,132},{128,196},{192,0},{4,64},{68,128},{132,192},{196,4... | collective-permute-start | bytes 294920 | tf_op jit(solution)/shard_map/ppermute | solution.py:20
  185.4 35.0 %copy-start = (f32[192,512]{1,0:T(8,128)S(1)}, f32[192,512]{1,0:T(8,128)}, u32[]{:S(2)}) copy-start(f32[192,512]{1,0:T(8,128)} %get-tuple-element.31) | copy-start | bytes 1179652
  185.4 20.0 %collective-permute-start.26 = (bf16[192,512]{1,0:T(8,128)(2,1)}, bf16[192,512]{1,0:T(8,128)(2,1)S(1)}, u32[]{:S(2)}, u32[]{:S(2)}) collective-permute-start(bf16[192,512]{1,0:T(8,128)(2,1)} %get-tuple-element.38), channel_id=1, source_target_pairs={{0,128},{64,192},{128,4},{192,68},{4,132},{68,196},{132,0},{196,64... | collective-permute-start | bytes 589832 | tf_op jit(solution)/shard_map/ppermute | solution.py:20
  188.7 16.7 %collective-permute-start.27 = (bf16[96,512]{1,0:T(8,128)(2,1)}, bf16[96,512]{1,0:T(8,128)(2,1)S(1)}, u32[]{:S(2)}, u32[]{:S(2)}) collective-permute-start(bf16[96,512]{1,0:T(8,128)(2,1)} %get-tuple-element.39), channel_id=1, source_target_pairs={{0,192},{64,4},{128,68},{192,132},{4,196},{68,0},{132,64},{196,128... | collective-permute-start | bytes 294920 | tf_op jit(solution)/shard_map/ppermute | solution.py:20
  189.3 21.1 %collective-permute-start.21 = (bf16[192,512]{1,0:T(8,128)(2,1)}, bf16[192,512]{1,0:T(8,128)(2,1)S(1)}, u32[]{:S(2)}, u32[]{:S(2)}) collective-permute-start(bf16[192,512]{1,0:T(8,128)(2,1)} %get-tuple-element.32), channel_id=1, source_target_pairs={{0,132},{64,196},{128,0},{192,64},{4,128},{68,192},{132,4},{196,68... | collective-permute-start | bytes 589832 | tf_op jit(solution)/shard_map/ppermute | solution.py:20
  191.2 21.4 %collective-permute-start.22 = (bf16[192,512]{1,0:T(8,128)(2,1)}, bf16[192,512]{1,0:T(8,128)(2,1)S(1)}, u32[]{:S(2)}, u32[]{:S(2)}) collective-permute-start(bf16[192,512]{1,0:T(8,128)(2,1)} %get-tuple-element.33), channel_id=1, source_target_pairs={{0,128},{64,192},{128,4},{192,68},{4,132},{68,196},{132,0},{196,64... | collective-permute-start | bytes 589832 | tf_op jit(solution)/shard_map/ppermute | solution.py:20
  194.5 18.1 %collective-permute-start.25 = (bf16[192,512]{1,0:T(8,128)(2,1)S(1)}, bf16[192,512]{1,0:T(8,128)(2,1)S(1)}, u32[]{:S(2)}, u32[]{:S(2)}) collective-permute-start(bf16[192,512]{1,0:T(8,128)(2,1)S(1)} %add_convert_fusion.2), channel_id=1, source_target_pairs={{0,196},{64,0},{128,64},{192,128},{4,192},{68,4},{132,68},{196,132... | collective-permute-start | bytes 589832 | tf_op jit(solution)/shard_map/ppermute | solution.py:20
  206.4 14.0 %collective-permute-start.28 = (bf16[192,512]{1,0:T(8,128)(2,1)S(1)}, bf16[192,512]{1,0:T(8,128)(2,1)S(1)}, u32[]{:S(2)}, u32[]{:S(2)}) collective-permute-start(bf16[192,512]{1,0:T(8,128)(2,1)S(1)} %add_convert_fusion.1), channel_id=1, source_target_pairs={{0,64},{64,128},{128,192},{192,4},{4,68},{68,132},{132,196},{196,0... | collective-permute-start | bytes 589832 | tf_op jit(solution)/shard_map/ppermute | solution.py:20
  206.8 21.6 %collective-permute-start.19 = (bf16[384,128]{1,0:T(8,128)(2,1)S(1)}, bf16[384,128]{1,0:T(8,128)(2,1)S(1)}, u32[]{:S(2)}, u32[]{:S(2)}) collective-permute-start(bf16[384,128]{1,0:T(8,128)(2,1)S(1)} %get-tuple-element.50), channel_id=1, source_target_pairs={{0,4},{4,0},{1,5},{5,1},{2,6},{6,2},{3,7},{7,3},{8,12},{12,8},{9,1... | collective-permute-start | bytes 294920 | tf_op jit(solution)/shard_map/ppermute | solution.py:28
  220.6 8.5 %collective-permute-start.29 = (bf16[192,128]{1,0:T(8,128)(2,1)S(1)}, bf16[192,128]{1,0:T(8,128)(2,1)S(1)}, u32[]{:S(2)}, u32[]{:S(2)}) collective-permute-start(bf16[192,128]{1,0:T(8,128)(2,1)S(1)} %get-tuple-element.46), channel_id=1, source_target_pairs={{0,3},{1,0},{2,1},{3,2},{4,7},{5,4},{6,5},{7,6},{8,11},{9,8},{10,9... | collective-permute-start | bytes 147464 | tf_op jit(solution)/shard_map/ppermute | solution.py:24
  226.1 5.6 %collective-permute-start.30 = (bf16[192,128]{1,0:T(8,128)(2,1)S(1)}, bf16[192,128]{1,0:T(8,128)(2,1)S(1)}, u32[]{:S(2)}, u32[]{:S(2)}) collective-permute-start(bf16[192,128]{1,0:T(8,128)(2,1)S(1)} %get-tuple-element.48), channel_id=1, source_target_pairs={{0,2},{1,3},{2,0},{3,1},{4,6},{5,7},{6,4},{7,5},{8,10},{9,11},{10,... | collective-permute-start | bytes 147464 | tf_op jit(solution)/shard_map/ppermute | solution.py:24
  227.0 5.3 %collective-permute-start.31 = (bf16[192,128]{1,0:T(8,128)(2,1)S(1)}, bf16[192,128]{1,0:T(8,128)(2,1)S(1)}, u32[]{:S(2)}, u32[]{:S(2)}) collective-permute-start(bf16[192,128]{1,0:T(8,128)(2,1)S(1)} %get-tuple-element.47), channel_id=1, source_target_pairs={{0,1},{1,2},{2,3},{3,0},{4,5},{5,6},{6,7},{7,4},{8,9},{9,10},{10,1... | collective-permute-start | bytes 147464 | tf_op jit(solution)/shard_map/ppermute | solution.py:24
where the time goes:
time: 233 us
  waiting for transfers between devices  114 us (49%)
  starting transfers between devices  75.2 us (32%)
  Pallas kernels  28.7 us (12%)
  local copies, waits for them, and re-layouts  8.94 us (4%)
  other arithmetic  5.28 us (2%)
    ppermute x12, waiting for transfers between devices, along(): return lax.ppermute(array, axis, [(k, (k + step) % 4) for k in range(4)])  39.3 us
    all_to_all x1, waiting for transfers between devices, step(): terms = lax.all_to_all(terms, PLANE, 0, 0, tiled=True)  36.6 us
    ppermute x16, waiting for transfers between devices, along_z(): lax.ppermute(array, ('zl', 'zh'), [(place(z), place((z + step) % 8)) for...  33.1 us
    pallas_call x4, Pallas kernels, kernel(): pl.pallas_call(body, in_specs=[spec_of[p] for p in places], out_specs=[vm...  28.7 us
    ppermute x16, starting transfers between devices, along_z(): lax.ppermute(array, ('zl', 'zh'), [(place(z), place((z + step) % 8)) for...  24.9 us
    ppermute x12, starting transfers between devices, along(): return lax.ppermute(array, axis, [(k, (k + step) % 4) for k in range(4)])  24.3 us
    all_to_all x1, starting transfers between devices, step(): terms = lax.all_to_all(terms, PLANE, 0, 0, tiled=True)  9.28 us
    ppermute x4, starting transfers between devices, swapped(): return lax.ppermute(array, axis, [(0, 1), (1, 0)])  9.17 us
  transfers between devices with their start and end apart: 34, of which 20 were waited for; matrix products, arithmetic and copies ran while one was open for 4% of the time, Pallas kernels for 4%

commit v1 on v0

--- a/solution.py
+++ b/solution.py
@@ -104,33 +104,28 @@
         copy.wait()
 
 
-def score_body(s, part, source, *refs, scale):
-    first = len(source.shape) == 4
-    if first:
-        queries, passages, scores, stats, sems = refs
-    else:
-        before, passages, scores, stats, sems = refs
-        queries = source
-    _, quarter, wide = part.shape
+def score_body(s, own, other, pieces, queries, passages, scores, stats, sems, *, scale):
+    _, quarter, wide = own.shape
     count, full = queries.shape
     rows, width = count // 4, full // 8
     copies = Copies(sems)
     ready = []
-    for d in range(4):
+    for c, part in enumerate((own, other)):
+        for d in range(4):
+            for h in range(2):
+                piece = part.at[jnp.where((s[0] >= d) == (h == 0), SLOT[d], SLOT[d + 4])]
+                at = pl.ds((4 * c + d) * quarter, quarter), pl.ds(h * wide, wide)
+                ready.append(copies.start(piece, passages.at[at]))
+    for x in range(4):
         for h in range(2):
-            piece = part.at[jnp.where((s[0] >= d) == (h == 0), SLOT[d], SLOT[d + 4])]
-            at = pl.ds(d * quarter, quarter), pl.ds(h * wide, wide)
-            ready.append(copies.start(piece, passages.at[at]))
-    if first:
-        for x in range(4):
-            for h in range(2):
-                for k in range(4):
-                    at = (h * 4 + k) * width
-                    queries[x * rows : (x + 1) * rows, at : at + width] = source[
-                        x * 4 + (s[1] + 4 - k) % 4, h
-                    ]
+            for k in range(4):
+                at = (h * 4 + k) * width
+                queries[x * rows : (x + 1) * rows, at : at + width] = pieces[
+                    x * 4 + (s[1] + 4 - k) % 4, h
+                ]
     block = 2 * quarter
     wing = count // 2
+    low, none = jnp.full((1, wing), -jnp.inf, F32), jnp.zeros((1, wing), F32)
     wait(ready)
 
     def chunk(k, found):
@@ -146,15 +141,7 @@
             fresh.append((top, total + jnp.sum(jnp.exp(values - top), axis=0, keepdims=True)))
         return tuple(fresh)
 
-    def wide_row(k, j):
-        return jnp.concatenate([before[4 * k + 2 * j + n : 4 * k + 2 * j + n + 1] for n in (0, 1)], 1)
-
-    if first:
-        low, none = jnp.full((1, wing), -jnp.inf, F32), jnp.zeros((1, wing), F32)
-        start = ((low, none), (low, none))
-    else:
-        start = tuple((wide_row(0, j), wide_row(1, j)) for j in range(2))
-    found = lax.fori_loop(0, 2, chunk, start)
+    found = lax.fori_loop(0, 4, chunk, ((low, none), (low, none)), unroll=UNROLL[0])
     for x in range(4):
         j, k = divmod(x, 2)
         at = slice(k * rows, (k + 1) * rows)
@@ -162,27 +149,27 @@
         stats[4 + x : 5 + x] = found[j][1][:, at]
 
 
-def scored(scalars, part, source, before, count, full):
-    half = 4 * part.shape[1]
-    first = source.ndim == 4
+UNROLL = (1, True, 2)
+
+
+def scored(scalars, own, other, pieces):
+    _, _, rows, width = pieces.shape
+    count, full, half = 4 * rows, 8 * width, 4 * own.shape[1]
 
     def body(*refs):
         score_body(*refs, scale=3.0 / math.sqrt(full))
 
-    out = [near((count, full), BF16)] if first else []
-    out += [
-        near((half, full), BF16),
-        near((half, count), F32),
-        near((8, count // 4), F32),
-    ]
-    args = (scalars, part, source) if first else (scalars, part, source, before)
-    return kernel(body, args, "shvv"[: len(args)], out, [], 8, 2 * half * count * full)
-
-
-def grad_body(s, s_own, s_other, *refs):
+    out = [near((count, full), BF16)]
+    out += [near((2 * half, full), BF16), near((2 * half, count), F32), near((8, rows), F32)]
+    return kernel(
+        body, (scalars, own, other, pieces), "shhv", out, [], 16, 4 * half * count * full
+    )
+
+
+def grad_body(s, scores, *refs):
     seen, refs = refs[:4], refs[4:]
-    queries, p_own, p_other, d_own, d_other, terms, gv, bv, dv, tv, sems = refs
-    half, count = s_own.shape
+    queries, passages, d_own, d_other, terms, gv, bv, dv, tv, sems = refs
+    half, count = scores.shape[0] // 2, scores.shape[1]
     full = queries.shape[1]
     block, quarter, rows, width = half // 2, half // 4, count // 4, full // 8
     logs, wanted = [], []
@@ -205,36 +192,33 @@
         spot = tv.at[x, :, pl.ds((h * 4 + k) * width, width)]
         return pltpu.make_async_copy(spot, piece, sems.at[4 + 8 * x + 4 * h + k])
 
-    for source, scores in enumerate((s_other, s_own)):
-
-        def one(b, _):
+    for source in range(2):
+
+        def one(b, _, source=source):
             for k in range(2):
-                base = s[2 + (1 - source) * 4 + 2 * b + k]
-                ids = base + lax.broadcasted_iota(jnp.int32, (quarter, 1), 0)
+                base = (1 - source) * half + b * block + k * quarter
+                place = (1 - source) * 4 + 2 * b + k
+                ids = s[2 + place] + lax.broadcasted_iota(jnp.int32, (quarter, 1), 0)
                 hit = (ids.astype(F32) == targets).astype(F32)
-                at = pl.ds(pl.multiple_of(b * block + k * quarter, quarter), quarter)
+                at = pl.ds(pl.multiple_of(base, quarter), quarter)
                 value = (jnp.exp(scores[at] - log_total) - hit).astype(BF16)
                 bv[k * quarter : (k + 1) * quarter] = value
-                at = source * half + b * block + k * quarter
-                at = pl.ds(pl.multiple_of(at, quarter), quarter)
                 for x in range(4):
                     gv[x, at] = value[:, x * rows : (x + 1) * rows]
             dv[2 * source + b] = dot(bv[...], queries[...], ((1,), (0,)))
             sent(source, b).start()
             return 0
 
-        lax.fori_loop(0, 2, one, 0, unroll=True)
+        lax.fori_loop(0, 2, one, 0, unroll=UNROLL[1])
 
     def another(x, _):
-        values = dot(gv[x, :half], p_other[...], ((0,), (0,)))
-        values += dot(gv[x, half:], p_own[...], ((0,), (0,)))
-        tv[x] = values.astype(BF16)
+        tv[x] = dot(gv[x], passages[...], ((0,), (0,))).astype(BF16)
         for h in range(2):
             for k in range(4):
                 leaving(x, h, k).start()
         return 0
 
-    lax.fori_loop(0, 4, another, 0)
+    lax.fori_loop(0, 4, another, 0, unroll=UNROLL[2])
     for source in range(2):
         for b in range(2):
             sent(source, b).wait()
@@ -244,8 +228,8 @@
                 leaving(x, h, k).wait()
 
 
-def gradients(scalars, s_own, s_other, seen, queries, p_own, p_other):
-    half, count = s_own.shape
+def gradients(scalars, scores, seen, queries, passages):
+    half, count = scores.shape[0] // 2, scores.shape[1]
     full = queries.shape[1]
     out = [
         far((half, full), F32),
@@ -258,8 +242,8 @@
         pltpu.VMEM((4, half // 2, full), F32),
         pltpu.VMEM((4, count // 4, full), BF16),
     ]
-    args = (scalars, s_own, s_other, *seen, queries, p_own, p_other)
-    return kernel(grad_body, args, "s" + 9 * "v", out, scratch, 40, 8 * half * count * full)
+    args = (scalars, scores, *seen, queries, passages)
+    return kernel(grad_body, args, "s" + 7 * "v", out, scratch, 40, 8 * half * count * full)
 
 
 def combine_body(s, own, theirs, *refs):
@@ -318,7 +302,6 @@
 def step(queries, passages, positive):
     rows, width = queries.shape
     half, quarter = rows // 2, rows // 4
-    full, count = 8 * width, 2 * rows
     x, y, c = (lax.axis_index(a) for a in ("x", "y", "c"))
     zl, zh = lax.axis_index("zl"), lax.axis_index("zh")
 
@@ -340,8 +323,7 @@
     first = (group * rows + y * quarter).reshape(8)
     scalars = jnp.concatenate([zl[None], y[None], first, x[None]]).astype(jnp.int32)
 
-    block_queries, p_own, s_own, half_stats = scored(scalars, own, pieces, None, count, full)
-    p_other, s_other, stats = scored(scalars, other, block_queries, half_stats, count, full)
+    block_queries, block_passages, scores, stats = scored(scalars, own, other, pieces)
     wanted = lax.dynamic_slice(positive, (zh * half,), (half,)).astype(F32)
     seen = [stats] + [along(stats, "y", d) for d in (1, 2, 3)]
     tops = functools.reduce(jnp.maximum, [part[:4] for part in seen])
@@ -349,9 +331,7 @@
     stats = jnp.concatenate([tops, totals, wanted[None]])
     seen = [stats] + [along(stats, "x", d) for d in (1, 2, 3)]
 
-    d_own, d_other, terms = gradients(
-        scalars, s_own, s_other, seen, block_queries, p_own, p_other
-    )
+    d_own, d_other, terms = gradients(scalars, scores, seen, block_queries, block_passages)
     theirs = swapped(d_other, "c")
     terms = lax.all_to_all(terms, PLANE, 0, 0, tiled=True)
     mine, down, up, d2, d3, d5, d6, low, high = combined(scalars, d_own, theirs)

time: 233 us -> 235 us (level)
  waiting for transfers between devices: 114 us -> 118 us
    ppermute x4, waiting for transfers between devices: 5.27 us -> 8.68 us  [swapped(): return lax.ppermute(array, axis, [(0, 1), (1, 0)])]
    pallas_call x4 -> x3, Pallas kernels: 28.7 us -> 26.8 us  [kernel(): pl.pallas_call(body, in_specs=[spec_of[p] for p in places], out_specs=[vm...]
  transfers between devices with their start and end apart: 34 -> 34, of which waited for: 20 -> 21; matrix products, arithmetic and copies ran while one was open for 4% -> 4% of each run, Pallas kernels for 4% -> 2%
where the time goes in v1:
time: 235 us
  waiting for transfers between devices  118 us (50%)
  starting transfers between devices  74.9 us (32%)
  Pallas kernels  26.8 us (11%)
  local copies, waits for them, and re-layouts  8.97 us (4%)
  other arithmetic  5.28 us (2%)
    ppermute x12, waiting for transfers between devices, along(): return lax.ppermute(array, axis, [(k, (k + step) % 4) for k in range(4)])  39.3 us
    all_to_all x1, waiting for transfers between devices, step(): terms = lax.all_to_all(terms, PLANE, 0, 0, tiled=True)  36.6 us
    ppermute x16, waiting for transfers between devices, along_z(): lax.ppermute(array, ('zl', 'zh'), [(place(z), place((z + step) % 8)) for...  33.2 us
    pallas_call x3, Pallas kernels, kernel(): pl.pallas_call(body, in_specs=[spec_of[p] for p in places], out_specs=[vm...  26.8 us
    ppermute x16, starting transfers between devices, along_z(): lax.ppermute(array, ('zl', 'zh'), [(place(z), place((z + step) % 8)) for...  24.6 us
    ppermute x12, starting transfers between devices, along(): return lax.ppermute(array, axis, [(k, (k + step) % 4) for k in range(4)])  24.3 us
    all_to_all x1, starting transfers between devices, step(): terms = lax.all_to_all(terms, PLANE, 0, 0, tiled=True)  9.28 us
    ppermute x4, starting transfers between devices, swapped(): return lax.ppermute(array, axis, [(0, 1), (1, 0)])  9.17 us
  transfers between devices with their start and end apart: 34, of which 21 were waited for; matrix products, arithmetic and copies ran while one was open for 4% of the time, Pallas kernels for 2%

profile of v1, /device:TPU:68, one launch (start us, length us, event | category | flops | bytes accessed | tf_op | source)
XLA Modules:
  0.0 234.6 jit_solution(16625168824057311462)
XLA Ops:
  0.6 1.0 dynamic-slice_bitcast_fusion
  1.6 5.5 %collective-permute-start.12 = (bf16[384,128]{1,0:T(8,128)(2,1)S(1)}, bf16[384,128]{1,0:T(8,128)(2,1)S(1)}, u32[]{:S(2)}, u32[]{:S(2)}) collective-permute-start(bf16[384,128]{1,0:T(8,128)(2,1)S(1)} %get-tuple-element.46), channel_id=1, source_target_pairs={{0,4},{4,0},{1,5},{5,1},{2,6},{6,2},{3,7},{7,3},{8,12},{12,8},{9,1... | collective-permute-start | bytes 294920 | tf_op jit(solution)/shard_map/ppermute | solution.py:28
  7.1 5.3 %collective-permute-done.12 = bf16[384,128]{1,0:T(8,128)(2,1)S(1)} collective-permute-done((bf16[384,128]{1,0:T(8,128)(2,1)S(1)}, bf16[384,128]{1,0:T(8,128)(2,1)S(1)}, u32[]{:S(2)}, u32[]{:S(2)}) %collective-permute-start.12) | collective-permute-done | bytes 98336 | tf_op jit(solution)/shard_map/ppermute | solution.py:28
  12.4 2.4 %broadcast_in_dim.23 = bf16[16,2,384,128]{3,2,1,0:T(8,128)(2,1)} broadcast(bf16[2,384,128]{2,1,0:T(8,128)(2,1)S(1)} %pad_maximum_fusion.1), dimensions={1,2,3} | broadcast | bytes 3342336 | tf_op jit(solution)/shard_map/broadcast_in_dim | solution.py:32
  14.7 7.6 %all-to-all-start = ((bf16[16,2,384,128]{3,2,1,0:T(8,128)(2,1)}), bf16[16,2,384,128]{3,2,1,0:T(8,128)(2,1)S(1)}, u32[]{:S(2)}, u32[]{:S(2)}) async-start(bf16[16,2,384,128]{3,2,1,0:T(8,128)(2,1)} %broadcast_in_dim.23), calls=%async_computation | async-start | bytes 6291456 | tf_op jit(solution)/shard_map/all_to_all | solution.py:33
  22.3 1.5 collective-permute-start
  23.9 2.7 %collective-permute-start.1 = (bf16[192,128]{1,0:T(8,128)(2,1)S(1)}, bf16[192,128]{1,0:T(8,128)(2,1)S(1)}, u32[]{:S(2)}, u32[]{:S(2)}) collective-permute-start(bf16[192,128]{1,0:T(8,128)(2,1)S(1)} %get-tuple-element.52), channel_id=1, source_target_pairs={{0,2},{1,3},{2,0},{3,1},{4,6},{5,7},{6,4},{7,5},{8,10},{9,11},{10,... | collective-permute-start | bytes 147464 | tf_op jit(solution)/shard_map/ppermute | solution.py:24
  26.6 1.5 collective-permute-start.2
  28.0 30.8 %collective-permute-done = bf16[192,128]{1,0:T(8,128)(2,1)S(1)} collective-permute-done((bf16[192,128]{1,0:T(8,128)(2,1)S(1)}, bf16[192,128]{1,0:T(8,128)(2,1)S(1)}, u32[]{:S(2)}, u32[]{:S(2)}) %collective-permute-start) | collective-permute-done | bytes 49184 | tf_op jit(solution)/shard_map/ppermute | solution.py:24
  60.1 1.6 collective-permute-start.3
  62.1 3.6 %collective-permute-done.3 = bf16[192,512]{1,0:T(8,128)(2,1)S(1)} collective-permute-done((bf16[192,512]{1,0:T(8,128)(2,1)S(1)}, bf16[192,512]{1,0:T(8,128)(2,1)S(1)}, u32[]{:S(2)}, u32[]{:S(2)}) %collective-permute-start.3) | collective-permute-done | bytes 196640 | tf_op jit(solution)/shard_map/ppermute | solution.py:20
  65.7 2.5 %collective-permute-start.5 = (bf16[192,512]{1,0:T(8,128)(2,1)S(1)}, bf16[192,512]{1,0:T(8,128)(2,1)S(1)}, u32[]{:S(2)}, u32[]{:S(2)}) collective-permute-start(bf16[192,512]{1,0:T(8,128)(2,1)S(1)} %collective-permute-done.3), channel_id=1, source_target_pairs={{0,64},{64,128},{128,192},{192,4},{4,68},{68,132},{132,196},{196,0... | collective-permute-start | bytes 589832 | tf_op jit(solution)/shard_map/ppermute | solution.py:20
  70.1 2.0 collective-permute-done.5
  72.1 4.0 %collective-permute-start.7 = (bf16[192,512]{1,0:T(8,128)(2,1)S(1)}, bf16[192,512]{1,0:T(8,128)(2,1)S(1)}, u32[]{:S(2)}, u32[]{:S(2)}) collective-permute-start(bf16[192,512]{1,0:T(8,128)(2,1)S(1)} %collective-permute-done.5), channel_id=1, source_target_pairs={{0,64},{64,128},{128,192},{192,4},{4,68},{68,132},{132,196},{196,0... | collective-permute-start | bytes 589832 | tf_op jit(solution)/shard_map/ppermute | solution.py:20
  78.1 2.3 collective-permute-done.7
  80.4 3.7 %collective-permute-start.9 = (bf16[96,512]{1,0:T(8,128)(2,1)S(1)}, bf16[96,512]{1,0:T(8,128)(2,1)S(1)}, u32[]{:S(2)}, u32[]{:S(2)}) collective-permute-start(bf16[96,512]{1,0:T(8,128)(2,1)S(1)} %slice.68), channel_id=1, source_target_pairs={{0,64},{64,128},{128,192},{192,4},{4,68},{68,132},{132,196},{196,0... | collective-permute-start | bytes 294920 | tf_op jit(solution)/shard_map/ppermute | solution.py:20
  84.0 0.8 collective-permute-done.8
  87.0 3.6 %collective-permute-done.10 = bf16[96,512]{1,0:T(8,128)(2,1)S(1)} collective-permute-done((bf16[96,512]{1,0:T(8,128)(2,1)S(1)}, bf16[96,512]{1,0:T(8,128)(2,1)S(1)}, u32[]{:S(2)}, u32[]{:S(2)}) %collective-permute-start.10) | collective-permute-done | bytes 98336 | tf_op jit(solution)/shard_map/ppermute | solution.py:20
  91.6 3.4 %collective-permute-done.11.refs_2_ = bf16[8,192,512]{2,1,0:T(8,128)(2,1)} collective-permute-done((bf16[8,192,512]{2,1,0:T(8,128)(2,1)}, bf16[8,192,512]{2,1,0:T(8,128)(2,1)}, u32[]{:S(2)}, u32[]{:S(2)}) %collective-permute-start.11) | collective-permute-done | bytes 1572896 | tf_op jit(solution)/shard_map/ppermute | solution.py:28
  95.0 9.7 %shard_map.50 = (bf16[1536,1024]{1,0:T(8,128)(2,1)S(1)}, bf16[1536,1024]{1,0:T(8,128)(2,1)S(1)}, f32[1536,1536]{1,0:T(8,128)S(1)}, f32[8,384]{1,0:T(8,128)S(1)}) custom-call(s32[11]{0:T(128)S(1)} %pad_add_fusion.1.refs_0_.s, bf16[8,192,512]{2,1,0:T(8,128)(2,1)} %bitcast.5.refs_1_, bf16[8,192,512]{2,1,0:T(8,128)(2,1)} %collective-permute-done.11.refs_2_, ...), custom_call_target="tpu_custom_call" | custom-call | flops 4831838208 | bytes 9437184 | tf_op jit(solution)/shard_map/pallas_call | solution.py:63
  105.1 5.0 %collective-permute-start.14 = (f32[8,384]{1,0:T(8,128)S(1)}, f32[8,384]{1,0:T(8,128)S(1)}, u32[]{:S(2)}, u32[]{:S(2)}) collective-permute-start(f32[8,384]{1,0:T(8,128)S(1)} %get-tuple-element.19), channel_id=1, source_target_pairs={{0,2},{1,3},{2,0},{3,1},{4,6},{5,7},{6,4},{7,5},{8,10},{9,11},{10,... | collective-permute-start | bytes 36872 | tf_op jit(solution)/shard_map/ppermute | solution.py:24
  110.1 2.5 %collective-permute-start.15 = (f32[8,384]{1,0:T(8,128)S(1)}, f32[8,384]{1,0:T(8,128)S(1)}, u32[]{:S(2)}, u32[]{:S(2)}) collective-permute-start(f32[8,384]{1,0:T(8,128)S(1)} %get-tuple-element.19), channel_id=1, source_target_pairs={{0,3},{1,0},{2,1},{3,2},{4,7},{5,4},{6,5},{7,6},{8,11},{9,8},{10,9... | collective-permute-start | bytes 36872 | tf_op jit(solution)/shard_map/ppermute | solution.py:24
  112.7 1.3 collective-permute-done.15
  114.2 1.6 collective-permute-start.17
  115.7 1.2 collective-permute-start.18
  116.9 1.0 collective-permute-done.16.refs_1_
  118.0 1.6 collective-permute-done.17.refs_2_
  119.6 0.7 collective-permute-done.18.refs_3_
  120.3 12.3 %shard_map.51 = (f32[768,1024]{1,0:T(8,128)}, f32[768,1024]{1,0:T(8,128)}, bf16[16,2,384,128]{3,2,1,0:T(8,128)(2,1)}) custom-call(s32[11]{0:T(128)S(1)} %pad_add_fusion.1.refs_0_.s, f32[1536,1536]{1,0:T(8,128)S(1)} %get-tuple-element.18.scores, f32[9,384]{1,0:T(8,128)S(1)} %pad_maximum_fusion.3.refs_0_, f32[9,384]{1,0:T(8,128)S(1)} %collective-permute-done.16.refs_1_, ...), custom_call_target="tpu_custom_call" | custom-call | flops 9663676416 | bytes 18874368 | tf_op jit(solution)/shard_map/pallas_call | solution.py:63
  132.7 9.3 %all-to-all-start.1 = ((bf16[16,2,384,128]{3,2,1,0:T(8,128)(2,1)}), bf16[16,2,384,128]{3,2,1,0:T(8,128)(2,1)S(1)}, u32[]{:S(2)}, u32[]{:S(2)}) async-start(bf16[16,2,384,128]{3,2,1,0:T(8,128)(2,1)} %get-tuple-element.22), calls=%async_computation.1 | async-start | bytes 6291456 | tf_op jit(solution)/shard_map/all_to_all | solution.py:336
  142.0 4.8 %shard_map.52 = (f32[192,512]{1,0:T(8,128)}, f32[192,512]{1,0:T(8,128)}, f32[192,512]{1,0:T(8,128)}, bf16[192,512]{1,0:T(8,128)(2,1)}, bf16[192,512]{1,0:T(8,128...) custom-call(s32[11]{0:T(128)S(1)} %pad_add_fusion.1.refs_0_.s, ...), custom_call_target="tpu_custom_call" | custom-call | flops 2147483648 | bytes 4194304 | tf_op jit(solution)/shard_map/pallas_call | solution.py:63
  147.1 2.7 %collective-permute-start.24 = (bf16[96,512]{1,0:T(8,128)(2,1)}, bf16[96,512]{1,0:T(8,128)(2,1)}, u32[]{:S(2)}, u32[]{:S(2)}) collective-permute-start(bf16[96,512]{1,0:T(8,128)(2,1)} %get-tuple-element.30), channel_id=1, source_target_pairs={{0,68},{64,132},{128,196},{192,0},{4,64},{68,128},{132,192},{196,4... | collective-permute-start | bytes 294920 | tf_op jit(solution)/shard_map/ppermute | solution.py:20
  149.8 36.6 %all-to-all-done.1 = bf16[16,2,384,128]{3,2,1,0:T(8,128)(2,1)S(1)} async-done(((bf16[16,2,384,128]{3,2,1,0:T(8,128)(2,1)}), bf16[16,2,384,128]{3,2,1,0:T(8,128)(2,1)S(1)}, u32[]{:S(2)}, u32[]{:S(2)}) %all-to-all-start.1) | async-done | bytes 3145760 | tf_op jit(solution)/shard_map/all_to_all | solution.py:336
  186.9 3.3 %collective-permute-start.26 = (bf16[192,512]{1,0:T(8,128)(2,1)}, bf16[192,512]{1,0:T(8,128)(2,1)S(1)}, u32[]{:S(2)}, u32[]{:S(2)}) collective-permute-start(bf16[192,512]{1,0:T(8,128)(2,1)} %get-tuple-element.32), channel_id=1, source_target_pairs={{0,128},{64,192},{128,4},{192,68},{4,132},{68,196},{132,0},{196,64... | collective-permute-start | bytes 589832 | tf_op jit(solution)/shard_map/ppermute | solution.py:20
  190.8 1.8 collective-permute-start.21
  192.6 2.3 collective-permute-start.22
  194.9 1.1 add_convert_fusion.2
  196.0 0.9 collective-permute-start.25
  197.0 9.9 %collective-permute-done.27 = bf16[96,512]{1,0:T(8,128)(2,1)S(1)} collective-permute-done((bf16[96,512]{1,0:T(8,128)(2,1)}, bf16[96,512]{1,0:T(8,128)(2,1)S(1)}, u32[]{:S(2)}, u32[]{:S(2)}) %collective-permute-start.27) | collective-permute-done | bytes 98336 | tf_op jit(solution)/shard_map/ppermute | solution.py:20
  206.8 1.1 add_convert_fusion.1
  208.3 3.6 %collective-permute-start.19 = (bf16[384,128]{1,0:T(8,128)(2,1)S(1)}, bf16[384,128]{1,0:T(8,128)(2,1)S(1)}, u32[]{:S(2)}, u32[]{:S(2)}) collective-permute-start(bf16[384,128]{1,0:T(8,128)(2,1)S(1)} %get-tuple-element.44), channel_id=1, source_target_pairs={{0,4},{4,0},{1,5},{5,1},{2,6},{6,2},{3,7},{7,3},{8,12},{12,8},{9,1... | collective-permute-start | bytes 294920 | tf_op jit(solution)/shard_map/ppermute | solution.py:28
  211.9 2.2 collective-permute-done.22
  214.1 7.8 %collective-permute-done.28 = bf16[192,512]{1,0:T(8,128)(2,1)S(1)} collective-permute-done((bf16[192,512]{1,0:T(8,128)(2,1)S(1)}, bf16[192,512]{1,0:T(8,128)(2,1)S(1)}, u32[]{:S(2)}, u32[]{:S(2)}) %collective-permute-start.28) | collective-permute-done | bytes 196640 | tf_op jit(solution)/shard_map/ppermute | solution.py:20
  222.1 5.5 %collective-permute-start.29 = (bf16[192,128]{1,0:T(8,128)(2,1)S(1)}, bf16[192,128]{1,0:T(8,128)(2,1)S(1)}, u32[]{:S(2)}, u32[]{:S(2)}) collective-permute-start(bf16[192,128]{1,0:T(8,128)(2,1)S(1)} %get-tuple-element.40), channel_id=1, source_target_pairs={{0,3},{1,0},{2,1},{3,2},{4,7},{5,4},{6,5},{7,6},{8,11},{9,8},{10,9... | collective-permute-start | bytes 147464 | tf_op jit(solution)/shard_map/ppermute | solution.py:24
  227.6 0.9 collective-permute-start.30
  228.5 1.3 collective-permute-start.31
  229.8 0.7 maximum_select_fusion
  230.6 2.6 %collective-permute-done.30 = bf16[192,128]{1,0:T(8,128)(2,1)S(1)} collective-permute-done((bf16[192,128]{1,0:T(8,128)(2,1)S(1)}, bf16[192,128]{1,0:T(8,128)(2,1)S(1)}, u32[]{:S(2)}, u32[]{:S(2)}) %collective-permute-start.30) | collective-permute-done | bytes 49184 | tf_op jit(solution)/shard_map/ppermute | solution.py:24
  (62 shorter events, 12.8 us)
Async XLA Ops:
  1.6 10.7 %collective-permute-start.12 = (bf16[384,128]{1,0:T(8,128)(2,1)S(1)}, bf16[384,128]{1,0:T(8,128)(2,1)S(1)}, u32[]{:S(2)}, u32[]{:S(2)}) collective-permute-start(bf16[384,128]{1,0:T(8,128)(2,1)S(1)} %get-tuple-element.46), channel_id=1, source_target_pairs={{0,4},{4,0},{1,5},{5,1},{2,6},{6,2},{3,7},{7,3},{8,12},{12,8},{9,1... | collective-permute-start | bytes 294920 | tf_op jit(solution)/shard_map/ppermute | solution.py:28
  14.7 7.6 %copy-start.1 = (bf16[768,128]{1,0:T(8,128)(2,1)S(1)}, bf16[768,128]{1,0:T(8,128)(2,1)}, u32[]{:S(2)}) copy-start(bf16[768,128]{1,0:T(8,128)(2,1)} %param.4) | copy-start | bytes 589828
  14.7 80.3 %all-to-all-start = ((bf16[16,2,384,128]{3,2,1,0:T(8,128)(2,1)}), bf16[16,2,384,128]{3,2,1,0:T(8,128)(2,1)S(1)}, u32[]{:S(2)}, u32[]{:S(2)}) async-start(bf16[16,2,384,128]{3,2,1,0:T(8,128)(2,1)} %broadcast_in_dim.23), calls=%async_computation | async-start | bytes 6291456 | tf_op jit(solution)/shard_map/all_to_all | solution.py:33
  22.3 36.4 %collective-permute-start = (bf16[192,128]{1,0:T(8,128)(2,1)S(1)}, bf16[192,128]{1,0:T(8,128)(2,1)S(1)}, u32[]{:S(2)}, u32[]{:S(2)}) collective-permute-start(bf16[192,128]{1,0:T(8,128)(2,1)S(1)} %get-tuple-element.50), channel_id=1, source_target_pairs={{0,1},{1,2},{2,3},{3,0},{4,5},{5,6},{6,7},{7,4},{8,9},{9,10},{10,1... | collective-permute-start | bytes 147464 | tf_op jit(solution)/shard_map/ppermute | solution.py:24
  23.9 34.9 %collective-permute-start.1 = (bf16[192,128]{1,0:T(8,128)(2,1)S(1)}, bf16[192,128]{1,0:T(8,128)(2,1)S(1)}, u32[]{:S(2)}, u32[]{:S(2)}) collective-permute-start(bf16[192,128]{1,0:T(8,128)(2,1)S(1)} %get-tuple-element.52), channel_id=1, source_target_pairs={{0,2},{1,3},{2,0},{3,1},{4,6},{5,7},{6,4},{7,5},{8,10},{9,11},{10,... | collective-permute-start | bytes 147464 | tf_op jit(solution)/shard_map/ppermute | solution.py:24
  26.6 32.8 %collective-permute-start.2 = (bf16[192,128]{1,0:T(8,128)(2,1)S(1)}, bf16[192,128]{1,0:T(8,128)(2,1)S(1)}, u32[]{:S(2)}, u32[]{:S(2)}) collective-permute-start(bf16[192,128]{1,0:T(8,128)(2,1)S(1)} %get-tuple-element.51), channel_id=1, source_target_pairs={{0,3},{1,0},{2,1},{3,2},{4,7},{5,4},{6,5},{7,6},{8,11},{9,8},{10,9... | collective-permute-start | bytes 147464 | tf_op jit(solution)/shard_map/ppermute | solution.py:24
  60.1 5.7 %collective-permute-start.3 = (bf16[192,512]{1,0:T(8,128)(2,1)S(1)}, bf16[192,512]{1,0:T(8,128)(2,1)S(1)}, u32[]{:S(2)}, u32[]{:S(2)}) collective-permute-start(bf16[192,512]{1,0:T(8,128)(2,1)S(1)} %get-tuple-element.47), channel_id=1, source_target_pairs={{0,64},{64,128},{128,192},{192,4},{4,68},{68,132},{132,196},{196,0... | collective-permute-start | bytes 589832 | tf_op jit(solution)/shard_map/ppermute | solution.py:20
  61.7 7.0 %collective-permute-start.4 = (bf16[192,512]{1,0:T(8,128)(2,1)S(1)}, bf16[192,512]{1,0:T(8,128)(2,1)S(1)}, u32[]{:S(2)}, u32[]{:S(2)}) collective-permute-start(bf16[192,512]{1,0:T(8,128)(2,1)S(1)} %get-tuple-element.47), channel_id=1, source_target_pairs={{0,196},{64,0},{128,64},{192,128},{4,192},{68,4},{132,68},{196,132... | collective-permute-start | bytes 589832 | tf_op jit(solution)/shard_map/ppermute | solution.py:20
  65.7 6.4 %collective-permute-start.5 = (bf16[192,512]{1,0:T(8,128)(2,1)S(1)}, bf16[192,512]{1,0:T(8,128)(2,1)S(1)}, u32[]{:S(2)}, u32[]{:S(2)}) collective-permute-start(bf16[192,512]{1,0:T(8,128)(2,1)S(1)} %collective-permute-done.3), channel_id=1, source_target_pairs={{0,64},{64,128},{128,192},{192,4},{4,68},{68,132},{132,196},{196,0... | collective-permute-start | bytes 589832 | tf_op jit(solution)/shard_map/ppermute | solution.py:20
  68.7 7.9 %collective-permute-start.6 = (bf16[192,512]{1,0:T(8,128)(2,1)S(1)}, bf16[192,512]{1,0:T(8,128)(2,1)S(1)}, u32[]{:S(2)}, u32[]{:S(2)}) collective-permute-start(bf16[192,512]{1,0:T(8,128)(2,1)S(1)} %collective-permute-done.4), channel_id=1, source_target_pairs={{0,196},{64,0},{128,64},{192,128},{4,192},{68,4},{132,68},{196,132... | collective-permute-start | bytes 589832 | tf_op jit(solution)/shard_map/ppermute | solution.py:20
  72.1 8.2 %collective-permute-start.7 = (bf16[192,512]{1,0:T(8,128)(2,1)S(1)}, bf16[192,512]{1,0:T(8,128)(2,1)S(1)}, u32[]{:S(2)}, u32[]{:S(2)}) collective-permute-start(bf16[192,512]{1,0:T(8,128)(2,1)S(1)} %collective-permute-done.5), channel_id=1, source_target_pairs={{0,64},{64,128},{128,192},{192,4},{4,68},{68,132},{132,196},{196,0... | collective-permute-start | bytes 589832 | tf_op jit(solution)/shard_map/ppermute | solution.py:20
  76.7 8.2 %collective-permute-start.8 = (bf16[192,512]{1,0:T(8,128)(2,1)S(1)}, bf16[192,512]{1,0:T(8,128)(2,1)S(1)}, u32[]{:S(2)}, u32[]{:S(2)}) collective-permute-start(bf16[192,512]{1,0:T(8,128)(2,1)S(1)} %collective-permute-done.6), channel_id=1, source_target_pairs={{0,196},{64,0},{128,64},{192,128},{4,192},{68,4},{132,68},{196,132... | collective-permute-start | bytes 589832 | tf_op jit(solution)/shard_map/ppermute | solution.py:20
  80.4 6.0 %collective-permute-start.9 = (bf16[96,512]{1,0:T(8,128)(2,1)S(1)}, bf16[96,512]{1,0:T(8,128)(2,1)S(1)}, u32[]{:S(2)}, u32[]{:S(2)}) collective-permute-start(bf16[96,512]{1,0:T(8,128)(2,1)S(1)} %slice.68), channel_id=1, source_target_pairs={{0,64},{64,128},{128,192},{192,4},{4,68},{68,132},{132,196},{196,0... | collective-permute-start | bytes 294920 | tf_op jit(solution)/shard_map/ppermute | solution.py:20
  84.9 5.7 %collective-permute-start.10 = (bf16[96,512]{1,0:T(8,128)(2,1)S(1)}, bf16[96,512]{1,0:T(8,128)(2,1)S(1)}, u32[]{:S(2)}, u32[]{:S(2)}) collective-permute-start(bf16[96,512]{1,0:T(8,128)(2,1)S(1)} %slice.69), channel_id=1, source_target_pairs={{0,196},{64,0},{128,64},{192,128},{4,192},{68,4},{132,68},{196,132... | collective-permute-start | bytes 294920 | tf_op jit(solution)/shard_map/ppermute | solution.py:20
  91.2 3.8 %collective-permute-start.11 = (bf16[8,192,512]{2,1,0:T(8,128)(2,1)}, bf16[8,192,512]{2,1,0:T(8,128)(2,1)}, u32[]{:S(2)}, u32[]{:S(2)}) collective-permute-start(bf16[8,192,512]{2,1,0:T(8,128)(2,1)} %bitcast.5.refs_1_), channel_id=1, source_target_pairs={{0,8},{8,0},{1,9},{9,1},{2,10},{10,2},{3,11},{11,3},{4,12},{12,4},... | collective-permute-start | bytes 4718600 | tf_op jit(solution)/shard_map/ppermute | solution.py:28
  91.6 21.1 %copy-start.2 = (s32[768]{0:T(1024)S(1)}, s32[768]{0:T(1024)}, u32[]{:S(2)}) copy-start(s32[768]{0:T(1024)} %param.5) | copy-start | bytes 9220
  104.7 8.1 %collective-permute-start.13 = (f32[8,384]{1,0:T(8,128)S(1)}, f32[8,384]{1,0:T(8,128)S(1)}, u32[]{:S(2)}, u32[]{:S(2)}) collective-permute-start(f32[8,384]{1,0:T(8,128)S(1)} %get-tuple-element.19), channel_id=1, source_target_pairs={{0,1},{1,2},{2,3},{3,0},{4,5},{5,6},{6,7},{7,4},{8,9},{9,10},{10,1... | collective-permute-start | bytes 36872 | tf_op jit(solution)/shard_map/ppermute | solution.py:24
  105.1 7.6 %collective-permute-start.14 = (f32[8,384]{1,0:T(8,128)S(1)}, f32[8,384]{1,0:T(8,128)S(1)}, u32[]{:S(2)}, u32[]{:S(2)}) collective-permute-start(f32[8,384]{1,0:T(8,128)S(1)} %get-tuple-element.19), channel_id=1, source_target_pairs={{0,2},{1,3},{2,0},{3,1},{4,6},{5,7},{6,4},{7,5},{8,10},{9,11},{10,... | collective-permute-start | bytes 36872 | tf_op jit(solution)/shard_map/ppermute | solution.py:24
  110.1 3.9 %collective-permute-start.15 = (f32[8,384]{1,0:T(8,128)S(1)}, f32[8,384]{1,0:T(8,128)S(1)}, u32[]{:S(2)}, u32[]{:S(2)}) collective-permute-start(f32[8,384]{1,0:T(8,128)S(1)} %get-tuple-element.19), channel_id=1, source_target_pairs={{0,3},{1,0},{2,1},{3,2},{4,7},{5,4},{6,5},{7,6},{8,11},{9,8},{10,9... | collective-permute-start | bytes 36872 | tf_op jit(solution)/shard_map/ppermute | solution.py:24
  114.1 3.9 %collective-permute-start.16 = (f32[9,384]{1,0:T(8,128)S(1)}, f32[9,384]{1,0:T(8,128)S(1)}, u32[]{:S(2)}, u32[]{:S(2)}) collective-permute-start(f32[9,384]{1,0:T(8,128)S(1)} %pad_maximum_fusion.3.refs_0_), channel_id=1, source_target_pairs={{0,16},{16,32},{32,48},{48,0},{1,17},{17,33},{33,49},{49,1},{2,18}... | collective-permute-start | bytes 41480 | tf_op jit(solution)/shard_map/ppermute | solution.py:24
  114.2 5.4 %collective-permute-start.17 = (f32[9,384]{1,0:T(8,128)S(1)}, f32[9,384]{1,0:T(8,128)S(1)}, u32[]{:S(2)}, u32[]{:S(2)}) collective-permute-start(f32[9,384]{1,0:T(8,128)S(1)} %pad_maximum_fusion.3.refs_0_), channel_id=1, source_target_pairs={{0,32},{16,48},{32,0},{48,16},{1,33},{17,49},{33,1},{49,17},{2,34}... | collective-permute-start | bytes 41480 | tf_op jit(solution)/shard_map/ppermute | solution.py:24
  115.7 4.6 %collective-permute-start.18 = (f32[9,384]{1,0:T(8,128)S(1)}, f32[9,384]{1,0:T(8,128)S(1)}, u32[]{:S(2)}, u32[]{:S(2)}) collective-permute-start(f32[9,384]{1,0:T(8,128)S(1)} %pad_maximum_fusion.3.refs_0_), channel_id=1, source_target_pairs={{0,48},{16,0},{32,16},{48,32},{1,49},{17,1},{33,17},{49,33},{2,50}... | collective-permute-start | bytes 41480 | tf_op jit(solution)/shard_map/ppermute | solution.py:24
  132.6 9.4 %collective-permute-start.20 = (f32[768,1024]{1,0:T(8,128)}, f32[768,1024]{1,0:T(8,128)}, u32[]{:S(2)}, u32[]{:S(2)}) collective-permute-start(f32[768,1024]{1,0:T(8,128)} %get-tuple-element.24), channel_id=1, source_target_pairs={{0,8},{8,0},{1,9},{9,1},{2,10},{10,2},{3,11},{11,3},{4,12},{12,4},... | collective-permute-start | bytes 9437192 | tf_op jit(solution)/shard_map/ppermute | solution.py:28
  132.7 53.7 %all-to-all-start.1 = ((bf16[16,2,384,128]{3,2,1,0:T(8,128)(2,1)}), bf16[16,2,384,128]{3,2,1,0:T(8,128)(2,1)S(1)}, u32[]{:S(2)}, u32[]{:S(2)}) async-start(bf16[16,2,384,128]{3,2,1,0:T(8,128)(2,1)} %get-tuple-element.22), calls=%async_computation.1 | async-start | bytes 6291456 | tf_op jit(solution)/shard_map/all_to_all | solution.py:336
  146.8 48.1 %collective-permute-start.23 = (bf16[192,512]{1,0:T(8,128)(2,1)}, bf16[192,512]{1,0:T(8,128)(2,1)S(1)}, u32[]{:S(2)}, u32[]{:S(2)}) collective-permute-start(bf16[192,512]{1,0:T(8,128)(2,1)} %get-tuple-element.29), channel_id=1, source_target_pairs={{0,132},{64,196},{128,0},{192,64},{4,128},{68,192},{132,4},{196,68... | collective-permute-start | bytes 589832 | tf_op jit(solution)/shard_map/ppermute | solution.py:20
  147.1 45.5 %collective-permute-start.24 = (bf16[96,512]{1,0:T(8,128)(2,1)}, bf16[96,512]{1,0:T(8,128)(2,1)}, u32[]{:S(2)}, u32[]{:S(2)}) collective-permute-start(bf16[96,512]{1,0:T(8,128)(2,1)} %get-tuple-element.30), channel_id=1, source_target_pairs={{0,68},{64,132},{128,196},{192,0},{4,64},{68,128},{132,192},{196,4... | collective-permute-start | bytes 294920 | tf_op jit(solution)/shard_map/ppermute | solution.py:20
  186.9 35.0 %copy-start = (f32[192,512]{1,0:T(8,128)S(1)}, f32[192,512]{1,0:T(8,128)}, u32[]{:S(2)}) copy-start(f32[192,512]{1,0:T(8,128)} %get-tuple-element.25) | copy-start | bytes 1179652
  186.9 20.0 %collective-permute-start.26 = (bf16[192,512]{1,0:T(8,128)(2,1)}, bf16[192,512]{1,0:T(8,128)(2,1)S(1)}, u32[]{:S(2)}, u32[]{:S(2)}) collective-permute-start(bf16[192,512]{1,0:T(8,128)(2,1)} %get-tuple-element.32), channel_id=1, source_target_pairs={{0,128},{64,192},{128,4},{192,68},{4,132},{68,196},{132,0},{196,64... | collective-permute-start | bytes 589832 | tf_op jit(solution)/shard_map/ppermute | solution.py:20
  190.2 16.6 %collective-permute-start.27 = (bf16[96,512]{1,0:T(8,128)(2,1)}, bf16[96,512]{1,0:T(8,128)(2,1)S(1)}, u32[]{:S(2)}, u32[]{:S(2)}) collective-permute-start(bf16[96,512]{1,0:T(8,128)(2,1)} %get-tuple-element.33), channel_id=1, source_target_pairs={{0,192},{64,4},{128,68},{192,132},{4,196},{68,0},{132,64},{196,128... | collective-permute-start | bytes 294920 | tf_op jit(solution)/shard_map/ppermute | solution.py:20
  190.8 21.1 %collective-permute-start.21 = (bf16[192,512]{1,0:T(8,128)(2,1)}, bf16[192,512]{1,0:T(8,128)(2,1)S(1)}, u32[]{:S(2)}, u32[]{:S(2)}) collective-permute-start(bf16[192,512]{1,0:T(8,128)(2,1)} %get-tuple-element.26), channel_id=1, source_target_pairs={{0,132},{64,196},{128,0},{192,64},{4,128},{68,192},{132,4},{196,68... | collective-permute-start | bytes 589832 | tf_op jit(solution)/shard_map/ppermute | solution.py:20
  192.6 21.4 %collective-permute-start.22 = (bf16[192,512]{1,0:T(8,128)(2,1)}, bf16[192,512]{1,0:T(8,128)(2,1)S(1)}, u32[]{:S(2)}, u32[]{:S(2)}) collective-permute-start(bf16[192,512]{1,0:T(8,128)(2,1)} %get-tuple-element.27), channel_id=1, source_target_pairs={{0,128},{64,192},{128,4},{192,68},{4,132},{68,196},{132,0},{196,64... | collective-permute-start | bytes 589832 | tf_op jit(solution)/shard_map/ppermute | solution.py:20
  196.0 18.1 %collective-permute-start.25 = (bf16[192,512]{1,0:T(8,128)(2,1)S(1)}, bf16[192,512]{1,0:T(8,128)(2,1)S(1)}, u32[]{:S(2)}, u32[]{:S(2)}) collective-permute-start(bf16[192,512]{1,0:T(8,128)(2,1)S(1)} %add_convert_fusion.2), channel_id=1, source_target_pairs={{0,196},{64,0},{128,64},{192,128},{4,192},{68,4},{132,68},{196,132... | collective-permute-start | bytes 589832 | tf_op jit(solution)/shard_map/ppermute | solution.py:20
  207.9 14.0 %collective-permute-start.28 = (bf16[192,512]{1,0:T(8,128)(2,1)S(1)}, bf16[192,512]{1,0:T(8,128)(2,1)S(1)}, u32[]{:S(2)}, u32[]{:S(2)}) collective-permute-start(bf16[192,512]{1,0:T(8,128)(2,1)S(1)} %add_convert_fusion.1), channel_id=1, source_target_pairs={{0,64},{64,128},{128,192},{192,4},{4,68},{68,132},{132,196},{196,0... | collective-permute-start | bytes 589832 | tf_op jit(solution)/shard_map/ppermute | solution.py:20
  208.3 21.6 %collective-permute-start.19 = (bf16[384,128]{1,0:T(8,128)(2,1)S(1)}, bf16[384,128]{1,0:T(8,128)(2,1)S(1)}, u32[]{:S(2)}, u32[]{:S(2)}) collective-permute-start(bf16[384,128]{1,0:T(8,128)(2,1)S(1)} %get-tuple-element.44), channel_id=1, source_target_pairs={{0,4},{4,0},{1,5},{5,1},{2,6},{6,2},{3,7},{7,3},{8,12},{12,8},{9,1... | collective-permute-start | bytes 294920 | tf_op jit(solution)/shard_map/ppermute | solution.py:28
  222.1 8.5 %collective-permute-start.29 = (bf16[192,128]{1,0:T(8,128)(2,1)S(1)}, bf16[192,128]{1,0:T(8,128)(2,1)S(1)}, u32[]{:S(2)}, u32[]{:S(2)}) collective-permute-start(bf16[192,128]{1,0:T(8,128)(2,1)S(1)} %get-tuple-element.40), channel_id=1, source_target_pairs={{0,3},{1,0},{2,1},{3,2},{4,7},{5,4},{6,5},{7,6},{8,11},{9,8},{10,9... | collective-permute-start | bytes 147464 | tf_op jit(solution)/shard_map/ppermute | solution.py:24
  227.6 5.6 %collective-permute-start.30 = (bf16[192,128]{1,0:T(8,128)(2,1)S(1)}, bf16[192,128]{1,0:T(8,128)(2,1)S(1)}, u32[]{:S(2)}, u32[]{:S(2)}) collective-permute-start(bf16[192,128]{1,0:T(8,128)(2,1)S(1)} %get-tuple-element.42), channel_id=1, source_target_pairs={{0,2},{1,3},{2,0},{3,1},{4,6},{5,7},{6,4},{7,5},{8,10},{9,11},{10,... | collective-permute-start | bytes 147464 | tf_op jit(solution)/shard_map/ppermute | solution.py:24
  228.5 5.3 %collective-permute-start.31 = (bf16[192,128]{1,0:T(8,128)(2,1)S(1)}, bf16[192,128]{1,0:T(8,128)(2,1)S(1)}, u32[]{:S(2)}, u32[]{:S(2)}) collective-permute-start(bf16[192,128]{1,0:T(8,128)(2,1)S(1)} %get-tuple-element.41), channel_id=1, source_target_pairs={{0,1},{1,2},{2,3},{3,0},{4,5},{5,6},{6,7},{7,4},{8,9},{9,10},{10,1... | collective-permute-start | bytes 147464 | tf_op jit(solution)/shard_map/ppermute | solution.py:24

commit v2 on v1

--- a/solution.py
+++ b/solution.py
@@ -26,11 +26,6 @@
 
 def swapped(array, axis):
     return lax.ppermute(array, axis, [(0, 1), (1, 0)])
-
-
-def to_plane(array):
-    copies = jnp.broadcast_to(array[None], (16, *array.shape))
-    return lax.all_to_all(copies, PLANE, 0, 0, tiled=True)
 
 
 def dot(a, b, dims):
@@ -50,7 +45,7 @@
 SLOT = (0, 1, 3, 5, 7, 6, 4, 2)
 
 
-def kernel(body, args, places, out_shape, scratch, copies, flops):
+def kernel(body, args, places, out_shape, scratch, copies, flops, aliases=None):
     hbm, vmem = pl.BlockSpec(memory_space=pl.ANY), pl.BlockSpec(memory_space=pltpu.VMEM)
     if not INTERPRET:
         args = [
@@ -70,6 +65,7 @@
         cost_estimate=pl.CostEstimate(
             flops=flops, transcendentals=0, bytes_accessed=flops // 512
         ),
+        input_output_aliases=aliases or {},
         interpret=INTERPRET,
     )(*args)
 
@@ -102,6 +98,18 @@
 def wait(copies):
     for copy in copies:
         copy.wait()
+
+
+def copies_of(array, place, before=None):
+    def body(source, *refs):
+        *_, out, sems = refs
+        copies = Copies(sems)
+        wait([copies.start(source, out.at[n, place]) for n in range(16)])
+
+    args = (array,) if before is None else (array, before)
+    out = [far((16, 2, *array.shape), array.dtype)]
+    aliases = None if before is None else {1: 0}
+    return kernel(body, args, "vh"[: len(args)], out, [], 16, 2**24, aliases)[0]
 
 
 def score_body(s, own, other, pieces, queries, passages, scores, stats, sems, *, scale):
@@ -307,8 +315,8 @@
 
     kept = lax.dynamic_slice(queries, (zh * half, 0), (half, width))
     sent = lax.dynamic_slice(queries, ((1 - zh) * half, 0), (half, width))
-    copies = jnp.stack([kept, swapped(sent, "zh")])
-    pieces = to_plane(copies)
+    copies = copies_of(swapped(sent, "zh"), 1, copies_of(kept, 0))
+    pieces = lax.all_to_all(copies, PLANE, 0, 0, tiled=True)
 
     mine = [
         lax.dynamic_slice(passages, ((y + d) % 4 * quarter, 0), (quarter, width)) for d in range(4)

time: 235 us -> 234 us (level)
  Pallas kernels: 26.8 us -> 29.5 us
  local copies, waits for them, and re-layouts: 8.97 us -> 6.62 us
    pallas_call x3 -> x5, Pallas kernels: 26.8 us -> 29.5 us  [kernel(): pl.pallas_call(body, in_specs=[spec_of[p] for p in places], out_specs=[vm...]
    broadcast_in_dim x1 -> x0, local copies, waits for them, and re-layouts: 2.36 us -> none  [to_plane(): copies = jnp.broadcast_to(array[None], (16, *array.shape))]
  transfers between devices with their start and end apart: 34 -> 34, of which waited for: 21 -> 21; matrix products, arithmetic and copies ran while one was open for 4% -> 4% of each run, Pallas kernels for 2% -> 3%
where the time goes in v2:
time: 234 us
  waiting for transfers between devices  116 us (50%)
  starting transfers between devices  74.9 us (32%)
  Pallas kernels  29.5 us (13%)
  local copies, waits for them, and re-layouts  6.62 us (3%)
  other arithmetic  5.26 us (2%)
    ppermute x12, waiting for transfers between devices, along(): return lax.ppermute(array, axis, [(k, (k + step) % 4) for k in range(4)])  39.3 us
    all_to_all x1, waiting for transfers between devices, step(): terms = lax.all_to_all(terms, PLANE, 0, 0, tiled=True)  36.6 us
    ppermute x16, waiting for transfers between devices, along_z(): lax.ppermute(array, ('zl', 'zh'), [(place(z), place((z + step) % 8)) for...  33.2 us
    pallas_call x5, Pallas kernels, kernel(): pl.pallas_call(body, in_specs=[spec_of[p] for p in places], out_specs=[vm...  29.5 us
    ppermute x16, starting transfers between devices, along_z(): lax.ppermute(array, ('zl', 'zh'), [(place(z), place((z + step) % 8)) for...  24.6 us
    ppermute x12, starting transfers between devices, along(): return lax.ppermute(array, axis, [(k, (k + step) % 4) for k in range(4)])  24.3 us
    all_to_all x1, starting transfers between devices, step(): terms = lax.all_to_all(terms, PLANE, 0, 0, tiled=True)  9.28 us
    ppermute x4, starting transfers between devices, swapped(): return lax.ppermute(array, axis, [(0, 1), (1, 0)])  9.17 us
  transfers between devices with their start and end apart: 34, of which 21 were waited for; matrix products, arithmetic and copies ran while one was open for 4% of the time, Pallas kernels for 3%

profile of v2, /device:TPU:68, one launch (start us, length us, event | category | flops | bytes accessed | tf_op | source)
XLA Modules:
  0.0 233.6 jit_solution(17913142175736221695)
XLA Ops:
  0.6 1.0 constant_dynamic-slice_fusion
  1.6 5.5 %collective-permute-start.12 = (bf16[384,128]{1,0:T(8,128)(2,1)S(1)}, bf16[384,128]{1,0:T(8,128)(2,1)S(1)}, u32[]{:S(2)}, u32[]{:S(2)}) collective-permute-start(bf16[384,128]{1,0:T(8,128)(2,1)S(1)} %get-tuple-element.46), channel_id=1, source_target_pairs={{0,4},{4,0},{1,5},{5,1},{2,6},{6,2},{3,7},{7,3},{8,12},{12,8},{9,1... | collective-permute-start | bytes 294920 | tf_op jit(solution)/shard_map/ppermute | solution.py:28
  7.1 1.3 shard_map.50.refs_0_
  8.4 3.9 %collective-permute-done.12.source = bf16[384,128]{1,0:T(8,128)(2,1)S(1)} collective-permute-done((bf16[384,128]{1,0:T(8,128)(2,1)S(1)}, bf16[384,128]{1,0:T(8,128)(2,1)S(1)}, u32[]{:S(2)}, u32[]{:S(2)}) %collective-permute-start.12) | collective-permute-done | bytes 98336 | tf_op jit(solution)/shard_map/ppermute | solution.py:28
  12.3 1.4 shard_map.51
  13.7 7.6 %all-to-all-start = ((bf16[16,2,384,128]{3,2,1,0:T(8,128)(2,1)}), bf16[16,2,384,128]{3,2,1,0:T(8,128)(2,1)S(1)}, u32[]{:S(2)}, u32[]{:S(2)}) async-start(bf16[16,2,384,128]{3,2,1,0:T(8,128)(2,1)} %shard_map.51), calls=%async_computation | async-start | bytes 6291456 | tf_op jit(solution)/shard_map/all_to_all | solution.py:319
  21.3 1.5 collective-permute-start
  22.9 2.7 %collective-permute-start.1 = (bf16[192,128]{1,0:T(8,128)(2,1)S(1)}, bf16[192,128]{1,0:T(8,128)(2,1)S(1)}, u32[]{:S(2)}, u32[]{:S(2)}) collective-permute-start(bf16[192,128]{1,0:T(8,128)(2,1)S(1)} %get-tuple-element.52), channel_id=1, source_target_pairs={{0,2},{1,3},{2,0},{3,1},{4,6},{5,7},{6,4},{7,5},{8,10},{9,11},{10,... | collective-permute-start | bytes 147464 | tf_op jit(solution)/shard_map/ppermute | solution.py:24
  25.6 1.5 collective-permute-start.2
  27.0 30.8 %collective-permute-done = bf16[192,128]{1,0:T(8,128)(2,1)S(1)} collective-permute-done((bf16[192,128]{1,0:T(8,128)(2,1)S(1)}, bf16[192,128]{1,0:T(8,128)(2,1)S(1)}, u32[]{:S(2)}, u32[]{:S(2)}) %collective-permute-start) | collective-permute-done | bytes 49184 | tf_op jit(solution)/shard_map/ppermute | solution.py:24
  59.1 1.6 collective-permute-start.3
  61.1 3.6 %collective-permute-done.3 = bf16[192,512]{1,0:T(8,128)(2,1)S(1)} collective-permute-done((bf16[192,512]{1,0:T(8,128)(2,1)S(1)}, bf16[192,512]{1,0:T(8,128)(2,1)S(1)}, u32[]{:S(2)}, u32[]{:S(2)}) %collective-permute-start.3) | collective-permute-done | bytes 196640 | tf_op jit(solution)/shard_map/ppermute | solution.py:20
  64.7 2.5 %collective-permute-start.5 = (bf16[192,512]{1,0:T(8,128)(2,1)S(1)}, bf16[192,512]{1,0:T(8,128)(2,1)S(1)}, u32[]{:S(2)}, u32[]{:S(2)}) collective-permute-start(bf16[192,512]{1,0:T(8,128)(2,1)S(1)} %collective-permute-done.3), channel_id=1, source_target_pairs={{0,64},{64,128},{128,192},{192,4},{4,68},{68,132},{132,196},{196,0... | collective-permute-start | bytes 589832 | tf_op jit(solution)/shard_map/ppermute | solution.py:20
  69.1 2.0 collective-permute-done.5
  71.1 4.0 %collective-permute-start.7 = (bf16[192,512]{1,0:T(8,128)(2,1)S(1)}, bf16[192,512]{1,0:T(8,128)(2,1)S(1)}, u32[]{:S(2)}, u32[]{:S(2)}) collective-permute-start(bf16[192,512]{1,0:T(8,128)(2,1)S(1)} %collective-permute-done.5), channel_id=1, source_target_pairs={{0,64},{64,128},{128,192},{192,4},{4,68},{68,132},{132,196},{196,0... | collective-permute-start | bytes 589832 | tf_op jit(solution)/shard_map/ppermute | solution.py:20
  77.1 2.3 collective-permute-done.7
  79.4 3.7 %collective-permute-start.9 = (bf16[96,512]{1,0:T(8,128)(2,1)S(1)}, bf16[96,512]{1,0:T(8,128)(2,1)S(1)}, u32[]{:S(2)}, u32[]{:S(2)}) collective-permute-start(bf16[96,512]{1,0:T(8,128)(2,1)S(1)} %slice.68), channel_id=1, source_target_pairs={{0,64},{64,128},{128,192},{192,4},{4,68},{68,132},{132,196},{196,0... | collective-permute-start | bytes 294920 | tf_op jit(solution)/shard_map/ppermute | solution.py:20
  83.0 0.8 collective-permute-done.8
  86.0 3.6 %collective-permute-done.10 = bf16[96,512]{1,0:T(8,128)(2,1)S(1)} collective-permute-done((bf16[96,512]{1,0:T(8,128)(2,1)S(1)}, bf16[96,512]{1,0:T(8,128)(2,1)S(1)}, u32[]{:S(2)}, u32[]{:S(2)}) %collective-permute-start.10) | collective-permute-done | bytes 98336 | tf_op jit(solution)/shard_map/ppermute | solution.py:20
  90.6 3.4 %collective-permute-done.11.refs_2_ = bf16[8,192,512]{2,1,0:T(8,128)(2,1)} collective-permute-done((bf16[8,192,512]{2,1,0:T(8,128)(2,1)}, bf16[8,192,512]{2,1,0:T(8,128)(2,1)}, u32[]{:S(2)}, u32[]{:S(2)}) %collective-permute-start.11) | collective-permute-done | bytes 1572896 | tf_op jit(solution)/shard_map/ppermute | solution.py:28
  94.0 9.7 %shard_map.52 = (bf16[1536,1024]{1,0:T(8,128)(2,1)S(1)}, bf16[1536,1024]{1,0:T(8,128)(2,1)S(1)}, f32[1536,1536]{1,0:T(8,128)S(1)}, f32[8,384]{1,0:T(8,128)S(1)}) custom-call(s32[11]{0:T(128)S(1)} %pad_add_fusion.1.refs_0_.s, bf16[8,192,512]{2,1,0:T(8,128)(2,1)} %bitcast.5.refs_1_, bf16[8,192,512]{2,1,0:T(8,128)(2,1)} %collective-permute-done.11.refs_2_, ...), custom_call_target="tpu_custom_call" | custom-call | flops 4831838208 | bytes 9437184 | tf_op jit(solution)/shard_map/pallas_call | solution.py:58
  104.1 5.0 %collective-permute-start.14 = (f32[8,384]{1,0:T(8,128)S(1)}, f32[8,384]{1,0:T(8,128)S(1)}, u32[]{:S(2)}, u32[]{:S(2)}) collective-permute-start(f32[8,384]{1,0:T(8,128)S(1)} %get-tuple-element.19), channel_id=1, source_target_pairs={{0,2},{1,3},{2,0},{3,1},{4,6},{5,7},{6,4},{7,5},{8,10},{9,11},{10,... | collective-permute-start | bytes 36872 | tf_op jit(solution)/shard_map/ppermute | solution.py:24
  109.1 2.5 %collective-permute-start.15 = (f32[8,384]{1,0:T(8,128)S(1)}, f32[8,384]{1,0:T(8,128)S(1)}, u32[]{:S(2)}, u32[]{:S(2)}) collective-permute-start(f32[8,384]{1,0:T(8,128)S(1)} %get-tuple-element.19), channel_id=1, source_target_pairs={{0,3},{1,0},{2,1},{3,2},{4,7},{5,4},{6,5},{7,6},{8,11},{9,8},{10,9... | collective-permute-start | bytes 36872 | tf_op jit(solution)/shard_map/ppermute | solution.py:24
  111.7 1.3 collective-permute-done.15
  113.2 1.6 collective-permute-start.17
  114.7 1.2 collective-permute-start.18
  115.9 1.0 collective-permute-done.16.refs_1_
  117.0 1.6 collective-permute-done.17.refs_2_
  119.3 12.3 %shard_map.53 = (f32[768,1024]{1,0:T(8,128)}, f32[768,1024]{1,0:T(8,128)}, bf16[16,2,384,128]{3,2,1,0:T(8,128)(2,1)}) custom-call(s32[11]{0:T(128)S(1)} %pad_add_fusion.1.refs_0_.s, f32[1536,1536]{1,0:T(8,128)S(1)} %get-tuple-element.18.scores, f32[9,384]{1,0:T(8,128)S(1)} %pad_maximum_fusion.2.refs_0_, f32[9,384]{1,0:T(8,128)S(1)} %collective-permute-done.16.refs_1_, ...), custom_call_target="tpu_custom_call" | custom-call | flops 9663676416 | bytes 18874368 | tf_op jit(solution)/shard_map/pallas_call | solution.py:58
  131.7 9.3 %all-to-all-start.1 = ((bf16[16,2,384,128]{3,2,1,0:T(8,128)(2,1)}), bf16[16,2,384,128]{3,2,1,0:T(8,128)(2,1)S(1)}, u32[]{:S(2)}, u32[]{:S(2)}) async-start(bf16[16,2,384,128]{3,2,1,0:T(8,128)(2,1)} %get-tuple-element.22), calls=%async_computation.1 | async-start | bytes 6291456 | tf_op jit(solution)/shard_map/all_to_all | solution.py:344
  141.0 4.8 %shard_map.54 = (f32[192,512]{1,0:T(8,128)}, f32[192,512]{1,0:T(8,128)}, f32[192,512]{1,0:T(8,128)}, bf16[192,512]{1,0:T(8,128)(2,1)}, bf16[192,512]{1,0:T(8,128...) custom-call(s32[11]{0:T(128)S(1)} %pad_add_fusion.1.refs_0_.s, ...), custom_call_target="tpu_custom_call" | custom-call | flops 2147483648 | bytes 4194304 | tf_op jit(solution)/shard_map/pallas_call | solution.py:58
  146.1 2.7 %collective-permute-start.24 = (bf16[96,512]{1,0:T(8,128)(2,1)}, bf16[96,512]{1,0:T(8,128)(2,1)}, u32[]{:S(2)}, u32[]{:S(2)}) collective-permute-start(bf16[96,512]{1,0:T(8,128)(2,1)} %get-tuple-element.30), channel_id=1, source_target_pairs={{0,68},{64,132},{128,196},{192,0},{4,64},{68,128},{132,192},{196,4... | collective-permute-start | bytes 294920 | tf_op jit(solution)/shard_map/ppermute | solution.py:20
  148.8 36.6 %all-to-all-done.1 = bf16[16,2,384,128]{3,2,1,0:T(8,128)(2,1)S(1)} async-done(((bf16[16,2,384,128]{3,2,1,0:T(8,128)(2,1)}), bf16[16,2,384,128]{3,2,1,0:T(8,128)(2,1)S(1)}, u32[]{:S(2)}, u32[]{:S(2)}) %all-to-all-start.1) | async-done | bytes 3145760 | tf_op jit(solution)/shard_map/all_to_all | solution.py:344
  185.9 3.3 %collective-permute-start.26 = (bf16[192,512]{1,0:T(8,128)(2,1)}, bf16[192,512]{1,0:T(8,128)(2,1)S(1)}, u32[]{:S(2)}, u32[]{:S(2)}) collective-permute-start(bf16[192,512]{1,0:T(8,128)(2,1)} %get-tuple-element.32), channel_id=1, source_target_pairs={{0,128},{64,192},{128,4},{192,68},{4,132},{68,196},{132,0},{196,64... | collective-permute-start | bytes 589832 | tf_op jit(solution)/shard_map/ppermute | solution.py:20
  189.8 1.9 collective-permute-start.21
  191.6 2.3 collective-permute-start.22
  193.9 1.1 add_convert_fusion.2
  195.0 0.9 collective-permute-start.25
  196.0 9.9 %collective-permute-done.27 = bf16[96,512]{1,0:T(8,128)(2,1)S(1)} collective-permute-done((bf16[96,512]{1,0:T(8,128)(2,1)}, bf16[96,512]{1,0:T(8,128)(2,1)S(1)}, u32[]{:S(2)}, u32[]{:S(2)}) %collective-permute-start.27) | collective-permute-done | bytes 98336 | tf_op jit(solution)/shard_map/ppermute | solution.py:20
  205.8 1.1 add_convert_fusion.1
  207.3 3.6 %collective-permute-start.19 = (bf16[384,128]{1,0:T(8,128)(2,1)S(1)}, bf16[384,128]{1,0:T(8,128)(2,1)S(1)}, u32[]{:S(2)}, u32[]{:S(2)}) collective-permute-start(bf16[384,128]{1,0:T(8,128)(2,1)S(1)} %get-tuple-element.44), channel_id=1, source_target_pairs={{0,4},{4,0},{1,5},{5,1},{2,6},{6,2},{3,7},{7,3},{8,12},{12,8},{9,1... | collective-permute-start | bytes 294920 | tf_op jit(solution)/shard_map/ppermute | solution.py:28
  210.9 2.2 collective-permute-done.22
  213.1 7.8 %collective-permute-done.28 = bf16[192,512]{1,0:T(8,128)(2,1)S(1)} collective-permute-done((bf16[192,512]{1,0:T(8,128)(2,1)S(1)}, bf16[192,512]{1,0:T(8,128)(2,1)S(1)}, u32[]{:S(2)}, u32[]{:S(2)}) %collective-permute-start.28) | collective-permute-done | bytes 196640 | tf_op jit(solution)/shard_map/ppermute | solution.py:20
  221.1 5.5 %collective-permute-start.29 = (bf16[192,128]{1,0:T(8,128)(2,1)S(1)}, bf16[192,128]{1,0:T(8,128)(2,1)S(1)}, u32[]{:S(2)}, u32[]{:S(2)}) collective-permute-start(bf16[192,128]{1,0:T(8,128)(2,1)S(1)} %get-tuple-element.40), channel_id=1, source_target_pairs={{0,3},{1,0},{2,1},{3,2},{4,7},{5,4},{6,5},{7,6},{8,11},{9,8},{10,9... | collective-permute-start | bytes 147464 | tf_op jit(solution)/shard_map/ppermute | solution.py:24
  226.6 0.9 collective-permute-start.30
  227.5 1.3 collective-permute-start.31
  228.8 0.7 maximum_select_fusion
  229.6 2.6 %collective-permute-done.30 = bf16[192,128]{1,0:T(8,128)(2,1)S(1)} collective-permute-done((bf16[192,128]{1,0:T(8,128)(2,1)S(1)}, bf16[192,128]{1,0:T(8,128)(2,1)S(1)}, u32[]{:S(2)}, u32[]{:S(2)}) %collective-permute-start.30) | collective-permute-done | bytes 49184 | tf_op jit(solution)/shard_map/ppermute | solution.py:24
  (62 shorter events, 13.5 us)
Async XLA Ops:
  1.6 10.7 %collective-permute-start.12 = (bf16[384,128]{1,0:T(8,128)(2,1)S(1)}, bf16[384,128]{1,0:T(8,128)(2,1)S(1)}, u32[]{:S(2)}, u32[]{:S(2)}) collective-permute-start(bf16[384,128]{1,0:T(8,128)(2,1)S(1)} %get-tuple-element.46), channel_id=1, source_target_pairs={{0,4},{4,0},{1,5},{5,1},{2,6},{6,2},{3,7},{7,3},{8,12},{12,8},{9,1... | collective-permute-start | bytes 294920 | tf_op jit(solution)/shard_map/ppermute | solution.py:28
  13.7 7.6 %copy-start.1 = (bf16[768,128]{1,0:T(8,128)(2,1)S(1)}, bf16[768,128]{1,0:T(8,128)(2,1)}, u32[]{:S(2)}) copy-start(bf16[768,128]{1,0:T(8,128)(2,1)} %param.4) | copy-start | bytes 589828
  13.7 80.3 %all-to-all-start = ((bf16[16,2,384,128]{3,2,1,0:T(8,128)(2,1)}), bf16[16,2,384,128]{3,2,1,0:T(8,128)(2,1)S(1)}, u32[]{:S(2)}, u32[]{:S(2)}) async-start(bf16[16,2,384,128]{3,2,1,0:T(8,128)(2,1)} %shard_map.51), calls=%async_computation | async-start | bytes 6291456 | tf_op jit(solution)/shard_map/all_to_all | solution.py:319
  21.3 36.4 %collective-permute-start = (bf16[192,128]{1,0:T(8,128)(2,1)S(1)}, bf16[192,128]{1,0:T(8,128)(2,1)S(1)}, u32[]{:S(2)}, u32[]{:S(2)}) collective-permute-start(bf16[192,128]{1,0:T(8,128)(2,1)S(1)} %get-tuple-element.50), channel_id=1, source_target_pairs={{0,1},{1,2},{2,3},{3,0},{4,5},{5,6},{6,7},{7,4},{8,9},{9,10},{10,1... | collective-permute-start | bytes 147464 | tf_op jit(solution)/shard_map/ppermute | solution.py:24
  22.9 34.9 %collective-permute-start.1 = (bf16[192,128]{1,0:T(8,128)(2,1)S(1)}, bf16[192,128]{1,0:T(8,128)(2,1)S(1)}, u32[]{:S(2)}, u32[]{:S(2)}) collective-permute-start(bf16[192,128]{1,0:T(8,128)(2,1)S(1)} %get-tuple-element.52), channel_id=1, source_target_pairs={{0,2},{1,3},{2,0},{3,1},{4,6},{5,7},{6,4},{7,5},{8,10},{9,11},{10,... | collective-permute-start | bytes 147464 | tf_op jit(solution)/shard_map/ppermute | solution.py:24
  25.6 32.8 %collective-permute-start.2 = (bf16[192,128]{1,0:T(8,128)(2,1)S(1)}, bf16[192,128]{1,0:T(8,128)(2,1)S(1)}, u32[]{:S(2)}, u32[]{:S(2)}) collective-permute-start(bf16[192,128]{1,0:T(8,128)(2,1)S(1)} %get-tuple-element.51), channel_id=1, source_target_pairs={{0,3},{1,0},{2,1},{3,2},{4,7},{5,4},{6,5},{7,6},{8,11},{9,8},{10,9... | collective-permute-start | bytes 147464 | tf_op jit(solution)/shard_map/ppermute | solution.py:24
  59.1 5.7 %collective-permute-start.3 = (bf16[192,512]{1,0:T(8,128)(2,1)S(1)}, bf16[192,512]{1,0:T(8,128)(2,1)S(1)}, u32[]{:S(2)}, u32[]{:S(2)}) collective-permute-start(bf16[192,512]{1,0:T(8,128)(2,1)S(1)} %get-tuple-element.47), channel_id=1, source_target_pairs={{0,64},{64,128},{128,192},{192,4},{4,68},{68,132},{132,196},{196,0... | collective-permute-start | bytes 589832 | tf_op jit(solution)/shard_map/ppermute | solution.py:20
  60.7 7.0 %collective-permute-start.4 = (bf16[192,512]{1,0:T(8,128)(2,1)S(1)}, bf16[192,512]{1,0:T(8,128)(2,1)S(1)}, u32[]{:S(2)}, u32[]{:S(2)}) collective-permute-start(bf16[192,512]{1,0:T(8,128)(2,1)S(1)} %get-tuple-element.47), channel_id=1, source_target_pairs={{0,196},{64,0},{128,64},{192,128},{4,192},{68,4},{132,68},{196,132... | collective-permute-start | bytes 589832 | tf_op jit(solution)/shard_map/ppermute | solution.py:20
  64.7 6.4 %collective-permute-start.5 = (bf16[192,512]{1,0:T(8,128)(2,1)S(1)}, bf16[192,512]{1,0:T(8,128)(2,1)S(1)}, u32[]{:S(2)}, u32[]{:S(2)}) collective-permute-start(bf16[192,512]{1,0:T(8,128)(2,1)S(1)} %collective-permute-done.3), channel_id=1, source_target_pairs={{0,64},{64,128},{128,192},{192,4},{4,68},{68,132},{132,196},{196,0... | collective-permute-start | bytes 589832 | tf_op jit(solution)/shard_map/ppermute | solution.py:20
  67.7 7.9 %collective-permute-start.6 = (bf16[192,512]{1,0:T(8,128)(2,1)S(1)}, bf16[192,512]{1,0:T(8,128)(2,1)S(1)}, u32[]{:S(2)}, u32[]{:S(2)}) collective-permute-start(bf16[192,512]{1,0:T(8,128)(2,1)S(1)} %collective-permute-done.4), channel_id=1, source_target_pairs={{0,196},{64,0},{128,64},{192,128},{4,192},{68,4},{132,68},{196,132... | collective-permute-start | bytes 589832 | tf_op jit(solution)/shard_map/ppermute | solution.py:20
  71.1 8.2 %collective-permute-start.7 = (bf16[192,512]{1,0:T(8,128)(2,1)S(1)}, bf16[192,512]{1,0:T(8,128)(2,1)S(1)}, u32[]{:S(2)}, u32[]{:S(2)}) collective-permute-start(bf16[192,512]{1,0:T(8,128)(2,1)S(1)} %collective-permute-done.5), channel_id=1, source_target_pairs={{0,64},{64,128},{128,192},{192,4},{4,68},{68,132},{132,196},{196,0... | collective-permute-start | bytes 589832 | tf_op jit(solution)/shard_map/ppermute | solution.py:20
  75.7 8.2 %collective-permute-start.8 = (bf16[192,512]{1,0:T(8,128)(2,1)S(1)}, bf16[192,512]{1,0:T(8,128)(2,1)S(1)}, u32[]{:S(2)}, u32[]{:S(2)}) collective-permute-start(bf16[192,512]{1,0:T(8,128)(2,1)S(1)} %collective-permute-done.6), channel_id=1, source_target_pairs={{0,196},{64,0},{128,64},{192,128},{4,192},{68,4},{132,68},{196,132... | collective-permute-start | bytes 589832 | tf_op jit(solution)/shard_map/ppermute | solution.py:20
  79.4 6.0 %collective-permute-start.9 = (bf16[96,512]{1,0:T(8,128)(2,1)S(1)}, bf16[96,512]{1,0:T(8,128)(2,1)S(1)}, u32[]{:S(2)}, u32[]{:S(2)}) collective-permute-start(bf16[96,512]{1,0:T(8,128)(2,1)S(1)} %slice.68), channel_id=1, source_target_pairs={{0,64},{64,128},{128,192},{192,4},{4,68},{68,132},{132,196},{196,0... | collective-permute-start | bytes 294920 | tf_op jit(solution)/shard_map/ppermute | solution.py:20
  83.9 5.7 %collective-permute-start.10 = (bf16[96,512]{1,0:T(8,128)(2,1)S(1)}, bf16[96,512]{1,0:T(8,128)(2,1)S(1)}, u32[]{:S(2)}, u32[]{:S(2)}) collective-permute-start(bf16[96,512]{1,0:T(8,128)(2,1)S(1)} %slice.69), channel_id=1, source_target_pairs={{0,196},{64,0},{128,64},{192,128},{4,192},{68,4},{132,68},{196,132... | collective-permute-start | bytes 294920 | tf_op jit(solution)/shard_map/ppermute | solution.py:20
  90.2 3.8 %collective-permute-start.11 = (bf16[8,192,512]{2,1,0:T(8,128)(2,1)}, bf16[8,192,512]{2,1,0:T(8,128)(2,1)}, u32[]{:S(2)}, u32[]{:S(2)}) collective-permute-start(bf16[8,192,512]{2,1,0:T(8,128)(2,1)} %bitcast.5.refs_1_), channel_id=1, source_target_pairs={{0,8},{8,0},{1,9},{9,1},{2,10},{10,2},{3,11},{11,3},{4,12},{12,4},... | collective-permute-start | bytes 4718600 | tf_op jit(solution)/shard_map/ppermute | solution.py:28
  90.6 21.1 %copy-start.2 = (s32[768]{0:T(1024)S(1)}, s32[768]{0:T(1024)}, u32[]{:S(2)}) copy-start(s32[768]{0:T(1024)} %param.5) | copy-start | bytes 9220
  103.7 8.1 %collective-permute-start.13 = (f32[8,384]{1,0:T(8,128)S(1)}, f32[8,384]{1,0:T(8,128)S(1)}, u32[]{:S(2)}, u32[]{:S(2)}) collective-permute-start(f32[8,384]{1,0:T(8,128)S(1)} %get-tuple-element.19), channel_id=1, source_target_pairs={{0,1},{1,2},{2,3},{3,0},{4,5},{5,6},{6,7},{7,4},{8,9},{9,10},{10,1... | collective-permute-start | bytes 36872 | tf_op jit(solution)/shard_map/ppermute | solution.py:24
  104.1 7.6 %collective-permute-start.14 = (f32[8,384]{1,0:T(8,128)S(1)}, f32[8,384]{1,0:T(8,128)S(1)}, u32[]{:S(2)}, u32[]{:S(2)}) collective-permute-start(f32[8,384]{1,0:T(8,128)S(1)} %get-tuple-element.19), channel_id=1, source_target_pairs={{0,2},{1,3},{2,0},{3,1},{4,6},{5,7},{6,4},{7,5},{8,10},{9,11},{10,... | collective-permute-start | bytes 36872 | tf_op jit(solution)/shard_map/ppermute | solution.py:24
  109.1 3.9 %collective-permute-start.15 = (f32[8,384]{1,0:T(8,128)S(1)}, f32[8,384]{1,0:T(8,128)S(1)}, u32[]{:S(2)}, u32[]{:S(2)}) collective-permute-start(f32[8,384]{1,0:T(8,128)S(1)} %get-tuple-element.19), channel_id=1, source_target_pairs={{0,3},{1,0},{2,1},{3,2},{4,7},{5,4},{6,5},{7,6},{8,11},{9,8},{10,9... | collective-permute-start | bytes 36872 | tf_op jit(solution)/shard_map/ppermute | solution.py:24
  113.1 3.9 %collective-permute-start.16 = (f32[9,384]{1,0:T(8,128)S(1)}, f32[9,384]{1,0:T(8,128)S(1)}, u32[]{:S(2)}, u32[]{:S(2)}) collective-permute-start(f32[9,384]{1,0:T(8,128)S(1)} %pad_maximum_fusion.2.refs_0_), channel_id=1, source_target_pairs={{0,16},{16,32},{32,48},{48,0},{1,17},{17,33},{33,49},{49,1},{2,18}... | collective-permute-start | bytes 41480 | tf_op jit(solution)/shard_map/ppermute | solution.py:24
  113.2 5.4 %collective-permute-start.17 = (f32[9,384]{1,0:T(8,128)S(1)}, f32[9,384]{1,0:T(8,128)S(1)}, u32[]{:S(2)}, u32[]{:S(2)}) collective-permute-start(f32[9,384]{1,0:T(8,128)S(1)} %pad_maximum_fusion.2.refs_0_), channel_id=1, source_target_pairs={{0,32},{16,48},{32,0},{48,16},{1,33},{17,49},{33,1},{49,17},{2,34}... | collective-permute-start | bytes 41480 | tf_op jit(solution)/shard_map/ppermute | solution.py:24
  114.7 4.6 %collective-permute-start.18 = (f32[9,384]{1,0:T(8,128)S(1)}, f32[9,384]{1,0:T(8,128)S(1)}, u32[]{:S(2)}, u32[]{:S(2)}) collective-permute-start(f32[9,384]{1,0:T(8,128)S(1)} %pad_maximum_fusion.2.refs_0_), channel_id=1, source_target_pairs={{0,48},{16,0},{32,16},{48,32},{1,49},{17,1},{33,17},{49,33},{2,50}... | collective-permute-start | bytes 41480 | tf_op jit(solution)/shard_map/ppermute | solution.py:24
  131.6 9.4 %collective-permute-start.20 = (f32[768,1024]{1,0:T(8,128)}, f32[768,1024]{1,0:T(8,128)}, u32[]{:S(2)}, u32[]{:S(2)}) collective-permute-start(f32[768,1024]{1,0:T(8,128)} %get-tuple-element.24), channel_id=1, source_target_pairs={{0,8},{8,0},{1,9},{9,1},{2,10},{10,2},{3,11},{11,3},{4,12},{12,4},... | collective-permute-start | bytes 9437192 | tf_op jit(solution)/shard_map/ppermute | solution.py:28
  131.7 53.7 %all-to-all-start.1 = ((bf16[16,2,384,128]{3,2,1,0:T(8,128)(2,1)}), bf16[16,2,384,128]{3,2,1,0:T(8,128)(2,1)S(1)}, u32[]{:S(2)}, u32[]{:S(2)}) async-start(bf16[16,2,384,128]{3,2,1,0:T(8,128)(2,1)} %get-tuple-element.22), calls=%async_computation.1 | async-start | bytes 6291456 | tf_op jit(solution)/shard_map/all_to_all | solution.py:344
  145.8 48.1 %collective-permute-start.23 = (bf16[192,512]{1,0:T(8,128)(2,1)}, bf16[192,512]{1,0:T(8,128)(2,1)S(1)}, u32[]{:S(2)}, u32[]{:S(2)}) collective-permute-start(bf16[192,512]{1,0:T(8,128)(2,1)} %get-tuple-element.29), channel_id=1, source_target_pairs={{0,132},{64,196},{128,0},{192,64},{4,128},{68,192},{132,4},{196,68... | collective-permute-start | bytes 589832 | tf_op jit(solution)/shard_map/ppermute | solution.py:20
  146.1 45.5 %collective-permute-start.24 = (bf16[96,512]{1,0:T(8,128)(2,1)}, bf16[96,512]{1,0:T(8,128)(2,1)}, u32[]{:S(2)}, u32[]{:S(2)}) collective-permute-start(bf16[96,512]{1,0:T(8,128)(2,1)} %get-tuple-element.30), channel_id=1, source_target_pairs={{0,68},{64,132},{128,196},{192,0},{4,64},{68,128},{132,192},{196,4... | collective-permute-start | bytes 294920 | tf_op jit(solution)/shard_map/ppermute | solution.py:20
  185.9 35.0 %copy-start = (f32[192,512]{1,0:T(8,128)S(1)}, f32[192,512]{1,0:T(8,128)}, u32[]{:S(2)}) copy-start(f32[192,512]{1,0:T(8,128)} %get-tuple-element.25) | copy-start | bytes 1179652
  185.9 20.0 %collective-permute-start.26 = (bf16[192,512]{1,0:T(8,128)(2,1)}, bf16[192,512]{1,0:T(8,128)(2,1)S(1)}, u32[]{:S(2)}, u32[]{:S(2)}) collective-permute-start(bf16[192,512]{1,0:T(8,128)(2,1)} %get-tuple-element.32), channel_id=1, source_target_pairs={{0,128},{64,192},{128,4},{192,68},{4,132},{68,196},{132,0},{196,64... | collective-permute-start | bytes 589832 | tf_op jit(solution)/shard_map/ppermute | solution.py:20
  189.2 16.6 %collective-permute-start.27 = (bf16[96,512]{1,0:T(8,128)(2,1)}, bf16[96,512]{1,0:T(8,128)(2,1)S(1)}, u32[]{:S(2)}, u32[]{:S(2)}) collective-permute-start(bf16[96,512]{1,0:T(8,128)(2,1)} %get-tuple-element.33), channel_id=1, source_target_pairs={{0,192},{64,4},{128,68},{192,132},{4,196},{68,0},{132,64},{196,128... | collective-permute-start | bytes 294920 | tf_op jit(solution)/shard_map/ppermute | solution.py:20
  189.8 21.1 %collective-permute-start.21 = (bf16[192,512]{1,0:T(8,128)(2,1)}, bf16[192,512]{1,0:T(8,128)(2,1)S(1)}, u32[]{:S(2)}, u32[]{:S(2)}) collective-permute-start(bf16[192,512]{1,0:T(8,128)(2,1)} %get-tuple-element.26), channel_id=1, source_target_pairs={{0,132},{64,196},{128,0},{192,64},{4,128},{68,192},{132,4},{196,68... | collective-permute-start | bytes 589832 | tf_op jit(solution)/shard_map/ppermute | solution.py:20
  191.6 21.4 %collective-permute-start.22 = (bf16[192,512]{1,0:T(8,128)(2,1)}, bf16[192,512]{1,0:T(8,128)(2,1)S(1)}, u32[]{:S(2)}, u32[]{:S(2)}) collective-permute-start(bf16[192,512]{1,0:T(8,128)(2,1)} %get-tuple-element.27), channel_id=1, source_target_pairs={{0,128},{64,192},{128,4},{192,68},{4,132},{68,196},{132,0},{196,64... | collective-permute-start | bytes 589832 | tf_op jit(solution)/shard_map/ppermute | solution.py:20
  195.0 18.1 %collective-permute-start.25 = (bf16[192,512]{1,0:T(8,128)(2,1)S(1)}, bf16[192,512]{1,0:T(8,128)(2,1)S(1)}, u32[]{:S(2)}, u32[]{:S(2)}) collective-permute-start(bf16[192,512]{1,0:T(8,128)(2,1)S(1)} %add_convert_fusion.2), channel_id=1, source_target_pairs={{0,196},{64,0},{128,64},{192,128},{4,192},{68,4},{132,68},{196,132... | collective-permute-start | bytes 589832 | tf_op jit(solution)/shard_map/ppermute | solution.py:20
  206.9 14.0 %collective-permute-start.28 = (bf16[192,512]{1,0:T(8,128)(2,1)S(1)}, bf16[192,512]{1,0:T(8,128)(2,1)S(1)}, u32[]{:S(2)}, u32[]{:S(2)}) collective-permute-start(bf16[192,512]{1,0:T(8,128)(2,1)S(1)} %add_convert_fusion.1), channel_id=1, source_target_pairs={{0,64},{64,128},{128,192},{192,4},{4,68},{68,132},{132,196},{196,0... | collective-permute-start | bytes 589832 | tf_op jit(solution)/shard_map/ppermute | solution.py:20
  207.3 21.6 %collective-permute-start.19 = (bf16[384,128]{1,0:T(8,128)(2,1)S(1)}, bf16[384,128]{1,0:T(8,128)(2,1)S(1)}, u32[]{:S(2)}, u32[]{:S(2)}) collective-permute-start(bf16[384,128]{1,0:T(8,128)(2,1)S(1)} %get-tuple-element.44), channel_id=1, source_target_pairs={{0,4},{4,0},{1,5},{5,1},{2,6},{6,2},{3,7},{7,3},{8,12},{12,8},{9,1... | collective-permute-start | bytes 294920 | tf_op jit(solution)/shard_map/ppermute | solution.py:28
  221.1 8.5 %collective-permute-start.29 = (bf16[192,128]{1,0:T(8,128)(2,1)S(1)}, bf16[192,128]{1,0:T(8,128)(2,1)S(1)}, u32[]{:S(2)}, u32[]{:S(2)}) collective-permute-start(bf16[192,128]{1,0:T(8,128)(2,1)S(1)} %get-tuple-element.40), channel_id=1, source_target_pairs={{0,3},{1,0},{2,1},{3,2},{4,7},{5,4},{6,5},{7,6},{8,11},{9,8},{10,9... | collective-permute-start | bytes 147464 | tf_op jit(solution)/shard_map/ppermute | solution.py:24
  226.6 5.6 %collective-permute-start.30 = (bf16[192,128]{1,0:T(8,128)(2,1)S(1)}, bf16[192,128]{1,0:T(8,128)(2,1)S(1)}, u32[]{:S(2)}, u32[]{:S(2)}) collective-permute-start(bf16[192,128]{1,0:T(8,128)(2,1)S(1)} %get-tuple-element.42), channel_id=1, source_target_pairs={{0,2},{1,3},{2,0},{3,1},{4,6},{5,7},{6,4},{7,5},{8,10},{9,11},{10,... | collective-permute-start | bytes 147464 | tf_op jit(solution)/shard_map/ppermute | solution.py:24
  227.5 5.3 %collective-permute-start.31 = (bf16[192,128]{1,0:T(8,128)(2,1)S(1)}, bf16[192,128]{1,0:T(8,128)(2,1)S(1)}, u32[]{:S(2)}, u32[]{:S(2)}) collective-permute-start(bf16[192,128]{1,0:T(8,128)(2,1)S(1)} %get-tuple-element.41), channel_id=1, source_target_pairs={{0,1},{1,2},{2,3},{3,0},{4,5},{5,6},{6,7},{7,4},{8,9},{9,10},{10,1... | collective-permute-start | bytes 147464 | tf_op jit(solution)/shard_map/ppermute | solution.py:24

commit v3 on v2

--- a/solution.py
+++ b/solution.py
@@ -157,7 +157,7 @@
         stats[4 + x : 5 + x] = found[j][1][:, at]
 
 
-UNROLL = (1, True, 2)
+UNROLL = (2, True, 2)
 
 
 def scored(scalars, own, other, pieces):
@@ -345,13 +345,15 @@
     mine, down, up, d2, d3, d5, d6, low, high = combined(scalars, d_own, theirs)
     low, high = along_z(low, -3), along_z(high, 3)
     d3, d5 = along_z(d3, -2), along_z(d5, 2)
-    d2, d6 = along_z(d2, -2), along_z(d6, 2)
+    d2, d6 = along_z(d2, -1), along_z(d6, 1)
     rest, rest_up = ((0, quarter // 2), (0, 0)), ((quarter // 2, 0), (0, 0))
-    down = (down + d3.astype(F32) + jnp.pad(low.astype(F32), rest)).astype(BF16)
-    up = (up + d5.astype(F32) + jnp.pad(high.astype(F32), rest_up)).astype(BF16)
+    low, high = jnp.pad(low, rest), jnp.pad(high, rest_up)
+    down = sum(part.astype(F32) for part in (d2, d3, low)) + down
+    up = sum(part.astype(F32) for part in (d6, d5, high)) + up
+    down, up = down.astype(BF16), up.astype(BF16)
     down, up = along_z(down, -1), along_z(up, 1)
     total = mine
-    for part in (d2, d6, down, up):
+    for part in (down, up):
         total += part.astype(F32)
     total = total.astype(BF16)
     slices = [total[:, k * width : (k + 1) * width] for k in range(4)]

time: 234 us -> 231 us (0.987)
  the two profiles are of different devices: /device:TPU:68 before, /device:TPU:4 now
where the time goes in v3:
time: 231 us; the launch traced here: 230 us
  waiting for transfers between devices  99.7 us (43%)
  starting transfers between devices  88.9 us (38%)
  Pallas kernels  29 us (13%)
  local copies, waits for them, and re-layouts  6.61 us (3%)
  other arithmetic  5.35 us (2%)
    ppermute x12, waiting for transfers between devices, along(): return lax.ppermute(array, axis, [(k, (k + step) % 4) for k in range(4)])  42.3 us
    ppermute x16, starting transfers between devices, along_z(): lax.ppermute(array, ('zl', 'zh'), [(place(z), place((z + step) % 8)) for...  35.6 us
    all_to_all x1, waiting for transfers between devices, step(): terms = lax.all_to_all(terms, PLANE, 0, 0, tiled=True)  31.4 us
    pallas_call x5, Pallas kernels, kernel(): pl.pallas_call(body, in_specs=[spec_of[p] for p in places], out_specs=[vm...  29 us
    ppermute x12, starting transfers between devices, along(): return lax.ppermute(array, axis, [(k, (k + step) % 4) for k in range(4)])  25.7 us
    ppermute x16, waiting for transfers between devices, along_z(): lax.ppermute(array, ('zl', 'zh'), [(place(z), place((z + step) % 8)) for...  21 us
    ppermute x4, starting transfers between devices, swapped(): return lax.ppermute(array, axis, [(0, 1), (1, 0)])  13.8 us
    all_to_all x1, starting transfers between devices, step(): pieces = lax.all_to_all(copies, PLANE, 0, 0, tiled=True)  7.6 us
  transfers between devices with their start and end apart: 34, of which 18 were waited for; matrix products, arithmetic and copies ran while one was open for 4% of the time, Pallas kernels for 3%

profile of v3, /device:TPU:4, one launch (start us, length us, event | category | flops | bytes accessed | tf_op | source)
XLA Modules:
  0.0 230.4 jit_solution(12761872673687075811)
XLA Ops:
  0.6 1.0 constant_dynamic-slice_fusion
  1.6 7.3 %collective-permute-start.12 = (bf16[384,128]{1,0:T(8,128)(2,1)S(1)}, bf16[384,128]{1,0:T(8,128)(2,1)S(1)}, u32[]{:S(2)}, u32[]{:S(2)}) collective-permute-start(bf16[384,128]{1,0:T(8,128)(2,1)S(1)} %get-tuple-element.46), channel_id=1, source_target_pairs={{0,4},{4,0},{1,5},{5,1},{2,6},{6,2},{3,7},{7,3},{8,12},{12,8},{9,1... | collective-permute-start | bytes 294920 | tf_op jit(solution)/shard_map/ppermute | solution.py:28
  8.9 1.3 shard_map.50.refs_0_
  10.2 1.5 collective-permute-done.12.source
  11.8 1.4 shard_map.51
  13.1 7.6 %all-to-all-start = ((bf16[16,2,384,128]{3,2,1,0:T(8,128)(2,1)}), bf16[16,2,384,128]{3,2,1,0:T(8,128)(2,1)S(1)}, u32[]{:S(2)}, u32[]{:S(2)}) async-start(bf16[16,2,384,128]{3,2,1,0:T(8,128)(2,1)} %shard_map.51), calls=%async_computation | async-start | bytes 6291456 | tf_op jit(solution)/shard_map/all_to_all | solution.py:319
  20.8 1.5 collective-permute-start
  22.3 2.7 %collective-permute-start.1 = (bf16[192,128]{1,0:T(8,128)(2,1)S(1)}, bf16[192,128]{1,0:T(8,128)(2,1)S(1)}, u32[]{:S(2)}, u32[]{:S(2)}) collective-permute-start(bf16[192,128]{1,0:T(8,128)(2,1)S(1)} %get-tuple-element.52), channel_id=1, source_target_pairs={{0,2},{1,3},{2,0},{3,1},{4,6},{5,7},{6,4},{7,5},{8,10},{9,11},{10,... | collective-permute-start | bytes 147464 | tf_op jit(solution)/shard_map/ppermute | solution.py:24
  25.0 1.5 collective-permute-start.2
  26.5 30.6 %collective-permute-done = bf16[192,128]{1,0:T(8,128)(2,1)S(1)} collective-permute-done((bf16[192,128]{1,0:T(8,128)(2,1)S(1)}, bf16[192,128]{1,0:T(8,128)(2,1)S(1)}, u32[]{:S(2)}, u32[]{:S(2)}) %collective-permute-start) | collective-permute-done | bytes 49184 | tf_op jit(solution)/shard_map/ppermute | solution.py:24
  57.1 1.3 collective-permute-done.2
  59.1 3.0 %collective-permute-start.3 = (bf16[192,512]{1,0:T(8,128)(2,1)S(1)}, bf16[192,512]{1,0:T(8,128)(2,1)S(1)}, u32[]{:S(2)}, u32[]{:S(2)}) collective-permute-start(bf16[192,512]{1,0:T(8,128)(2,1)S(1)} %get-tuple-element.47), channel_id=1, source_target_pairs={{0,64},{64,128},{128,192},{192,4},{4,68},{68,132},{132,196},{196,0... | collective-permute-start | bytes 589832 | tf_op jit(solution)/shard_map/ppermute | solution.py:20
  62.1 1.9 collective-permute-start.4
  64.0 4.4 %collective-permute-done.3 = bf16[192,512]{1,0:T(8,128)(2,1)S(1)} collective-permute-done((bf16[192,512]{1,0:T(8,128)(2,1)S(1)}, bf16[192,512]{1,0:T(8,128)(2,1)S(1)}, u32[]{:S(2)}, u32[]{:S(2)}) %collective-permute-start.3) | collective-permute-done | bytes 196640 | tf_op jit(solution)/shard_map/ppermute | solution.py:20
  68.4 3.2 %collective-permute-start.6 = (bf16[192,512]{1,0:T(8,128)(2,1)S(1)}, bf16[192,512]{1,0:T(8,128)(2,1)S(1)}, u32[]{:S(2)}, u32[]{:S(2)}) collective-permute-start(bf16[192,512]{1,0:T(8,128)(2,1)S(1)} %collective-permute-done.4), channel_id=1, source_target_pairs={{0,196},{64,0},{128,64},{192,128},{4,192},{68,4},{132,68},{196,132... | collective-permute-start | bytes 589832 | tf_op jit(solution)/shard_map/ppermute | solution.py:20
  73.0 2.2 collective-permute-done.5
  75.3 3.2 %collective-permute-start.8 = (bf16[192,512]{1,0:T(8,128)(2,1)S(1)}, bf16[192,512]{1,0:T(8,128)(2,1)S(1)}, u32[]{:S(2)}, u32[]{:S(2)}) collective-permute-start(bf16[192,512]{1,0:T(8,128)(2,1)S(1)} %collective-permute-done.6), channel_id=1, source_target_pairs={{0,196},{64,0},{128,64},{192,128},{4,192},{68,4},{132,68},{196,132... | collective-permute-start | bytes 589832 | tf_op jit(solution)/shard_map/ppermute | solution.py:20
  79.9 2.2 collective-permute-done.7
  82.3 3.3 %collective-permute-start.10 = (bf16[96,512]{1,0:T(8,128)(2,1)S(1)}, bf16[96,512]{1,0:T(8,128)(2,1)S(1)}, u32[]{:S(2)}, u32[]{:S(2)}) collective-permute-start(bf16[96,512]{1,0:T(8,128)(2,1)S(1)} %slice.69), channel_id=1, source_target_pairs={{0,196},{64,0},{128,64},{192,128},{4,192},{68,4},{132,68},{196,132... | collective-permute-start | bytes 294920 | tf_op jit(solution)/shard_map/ppermute | solution.py:20
  86.9 1.1 collective-permute-done.9
  89.7 3.4 %collective-permute-done.11.refs_2_ = bf16[8,192,512]{2,1,0:T(8,128)(2,1)} collective-permute-done((bf16[8,192,512]{2,1,0:T(8,128)(2,1)}, bf16[8,192,512]{2,1,0:T(8,128)(2,1)}, u32[]{:S(2)}, u32[]{:S(2)}) %collective-permute-start.11) | collective-permute-done | bytes 1572896 | tf_op jit(solution)/shard_map/ppermute | solution.py:28
  93.1 9.2 %shard_map.52 = (bf16[1536,1024]{1,0:T(8,128)(2,1)S(1)}, bf16[1536,1024]{1,0:T(8,128)(2,1)S(1)}, f32[1536,1536]{1,0:T(8,128)S(1)}, f32[8,384]{1,0:T(8,128)S(1)}) custom-call(s32[11]{0:T(128)S(1)} %pad_add_fusion.1.refs_0_.s, bf16[8,192,512]{2,1,0:T(8,128)(2,1)} %bitcast.5.refs_1_, bf16[8,192,512]{2,1,0:T(8,128)(2,1)} %collective-permute-done.11.refs_2_, ...), custom_call_target="tpu_custom_call" | custom-call | flops 4831838208 | bytes 9437184 | tf_op jit(solution)/shard_map/pallas_call | solution.py:58
  102.4 6.5 %collective-permute-start.14 = (f32[8,384]{1,0:T(8,128)S(1)}, f32[8,384]{1,0:T(8,128)S(1)}, u32[]{:S(2)}, u32[]{:S(2)}) collective-permute-start(f32[8,384]{1,0:T(8,128)S(1)} %get-tuple-element.19), channel_id=1, source_target_pairs={{0,2},{1,3},{2,0},{3,1},{4,6},{5,7},{6,4},{7,5},{8,10},{9,11},{10,... | collective-permute-start | bytes 36872 | tf_op jit(solution)/shard_map/ppermute | solution.py:24
  109.3 1.4 collective-permute-done.14
  110.7 1.9 collective-permute-done.15
  112.6 1.9 collective-permute-start.16
  114.6 4.1 %collective-permute-start.17 = (f32[9,384]{1,0:T(8,128)S(1)}, f32[9,384]{1,0:T(8,128)S(1)}, u32[]{:S(2)}, u32[]{:S(2)}) collective-permute-start(f32[9,384]{1,0:T(8,128)S(1)} %pad_maximum_fusion.2.refs_0_), channel_id=1, source_target_pairs={{0,32},{16,48},{32,0},{48,16},{1,33},{17,49},{33,1},{49,17},{2,34}... | collective-permute-start | bytes 41480 | tf_op jit(solution)/shard_map/ppermute | solution.py:24
  119.0 1.7 collective-permute-done.17.refs_2_
  120.7 1.8 collective-permute-done.18.refs_3_
  122.5 12.3 %shard_map.53 = (f32[768,1024]{1,0:T(8,128)}, f32[768,1024]{1,0:T(8,128)}, bf16[16,2,384,128]{3,2,1,0:T(8,128)(2,1)}) custom-call(s32[11]{0:T(128)S(1)} %pad_add_fusion.1.refs_0_.s, f32[1536,1536]{1,0:T(8,128)S(1)} %get-tuple-element.18.scores, f32[9,384]{1,0:T(8,128)S(1)} %pad_maximum_fusion.2.refs_0_, f32[9,384]{1,0:T(8,128)S(1)} %collective-permute-done.16.refs_1_, ...), custom_call_target="tpu_custom_call" | custom-call | flops 9663676416 | bytes 18874368 | tf_op jit(solution)/shard_map/pallas_call | solution.py:58
  134.9 6.2 %all-to-all-start.1 = ((bf16[16,2,384,128]{3,2,1,0:T(8,128)(2,1)}), bf16[16,2,384,128]{3,2,1,0:T(8,128)(2,1)S(1)}, u32[]{:S(2)}, u32[]{:S(2)}) async-start(bf16[16,2,384,128]{3,2,1,0:T(8,128)(2,1)} %get-tuple-element.22), calls=%async_computation.1 | async-start | bytes 6291456 | tf_op jit(solution)/shard_map/all_to_all | solution.py:344
  141.1 4.8 %shard_map.54 = (f32[192,512]{1,0:T(8,128)}, f32[192,512]{1,0:T(8,128)}, f32[192,512]{1,0:T(8,128)}, bf16[192,512]{1,0:T(8,128)(2,1)}, bf16[192,512]{1,0:T(8,128...) custom-call(s32[11]{0:T(128)S(1)} %pad_add_fusion.1.refs_0_.s, ...), custom_call_target="tpu_custom_call" | custom-call | flops 2147483648 | bytes 4194304 | tf_op jit(solution)/shard_map/pallas_call | solution.py:58
  145.9 2.7 %collective-permute-start.21 = (bf16[192,512]{1,0:T(8,128)(2,1)}, bf16[192,512]{1,0:T(8,128)(2,1)S(1)}, u32[]{:S(2)}, u32[]{:S(2)}) collective-permute-start(bf16[192,512]{1,0:T(8,128)(2,1)} %get-tuple-element.26), channel_id=1, source_target_pairs={{0,196},{64,0},{128,64},{192,128},{4,192},{68,4},{132,68},{196,132... | collective-permute-start | bytes 589832 | tf_op jit(solution)/shard_map/ppermute | solution.py:20
  149.2 4.9 %collective-permute-start.23 = (bf16[96,512]{1,0:T(8,128)(2,1)}, bf16[96,512]{1,0:T(8,128)(2,1)}, u32[]{:S(2)}, u32[]{:S(2)}) collective-permute-start(bf16[96,512]{1,0:T(8,128)(2,1)} %get-tuple-element.28), channel_id=1, source_target_pairs={{0,68},{64,132},{128,196},{192,0},{4,64},{68,128},{132,192},{196,4... | collective-permute-start | bytes 294920 | tf_op jit(solution)/shard_map/ppermute | solution.py:20
  154.1 31.4 %all-to-all-done.1 = bf16[16,2,384,128]{3,2,1,0:T(8,128)(2,1)S(1)} async-done(((bf16[16,2,384,128]{3,2,1,0:T(8,128)(2,1)}), bf16[16,2,384,128]{3,2,1,0:T(8,128)(2,1)S(1)}, u32[]{:S(2)}, u32[]{:S(2)}) %all-to-all-start.1) | async-done | bytes 3145760 | tf_op jit(solution)/shard_map/all_to_all | solution.py:344
  186.1 5.9 %collective-permute-start.26 = (bf16[192,512]{1,0:T(8,128)(2,1)}, bf16[192,512]{1,0:T(8,128)(2,1)S(1)}, u32[]{:S(2)}, u32[]{:S(2)}) collective-permute-start(bf16[192,512]{1,0:T(8,128)(2,1)} %get-tuple-element.31), channel_id=1, source_target_pairs={{0,128},{64,192},{128,4},{192,68},{4,132},{68,196},{132,0},{196,64... | collective-permute-start | bytes 589832 | tf_op jit(solution)/shard_map/ppermute | solution.py:20
  192.0 1.2 add_convert_fusion.2
  193.2 2.8 %collective-permute-start.24 = (bf16[192,512]{1,0:T(8,128)(2,1)S(1)}, bf16[192,512]{1,0:T(8,128)(2,1)S(1)}, u32[]{:S(2)}, u32[]{:S(2)}) collective-permute-start(bf16[192,512]{1,0:T(8,128)(2,1)S(1)} %add_convert_fusion.2), channel_id=1, source_target_pairs={{0,196},{64,0},{128,64},{192,128},{4,192},{68,4},{132,68},{196,132... | collective-permute-start | bytes 589832 | tf_op jit(solution)/shard_map/ppermute | solution.py:20
  196.0 9.1 %collective-permute-done.27 = bf16[96,512]{1,0:T(8,128)(2,1)S(1)} collective-permute-done((bf16[96,512]{1,0:T(8,128)(2,1)}, bf16[96,512]{1,0:T(8,128)(2,1)S(1)}, u32[]{:S(2)}, u32[]{:S(2)}) %collective-permute-start.27) | collective-permute-done | bytes 98336 | tf_op jit(solution)/shard_map/ppermute | solution.py:20
  205.1 2.0 collective-permute-done.26
  207.1 1.1 add_convert_fusion.1
  208.2 3.9 %collective-permute-start.28 = (bf16[192,512]{1,0:T(8,128)(2,1)S(1)}, bf16[192,512]{1,0:T(8,128)(2,1)S(1)}, u32[]{:S(2)}, u32[]{:S(2)}) collective-permute-start(bf16[192,512]{1,0:T(8,128)(2,1)S(1)} %add_convert_fusion.1), channel_id=1, source_target_pairs={{0,64},{64,128},{128,192},{192,4},{4,68},{68,132},{132,196},{196,0... | collective-permute-start | bytes 589832 | tf_op jit(solution)/shard_map/ppermute | solution.py:20
  212.0 6.4 %collective-permute-start.19 = (bf16[384,128]{1,0:T(8,128)(2,1)S(1)}, bf16[384,128]{1,0:T(8,128)(2,1)S(1)}, u32[]{:S(2)}, u32[]{:S(2)}) collective-permute-start(bf16[384,128]{1,0:T(8,128)(2,1)S(1)} %get-tuple-element.44), channel_id=1, source_target_pairs={{0,4},{4,0},{1,5},{5,1},{2,6},{6,2},{3,7},{7,3},{8,12},{12,8},{9,1... | collective-permute-start | bytes 294920 | tf_op jit(solution)/shard_map/ppermute | solution.py:28
  218.6 4.9 %collective-permute-start.29 = (bf16[192,128]{1,0:T(8,128)(2,1)S(1)}, bf16[192,128]{1,0:T(8,128)(2,1)S(1)}, u32[]{:S(2)}, u32[]{:S(2)}) collective-permute-start(bf16[192,128]{1,0:T(8,128)(2,1)S(1)} %get-tuple-element.40), channel_id=1, source_target_pairs={{0,3},{1,0},{2,1},{3,2},{4,7},{5,4},{6,5},{7,6},{8,11},{9,8},{10,9... | collective-permute-start | bytes 147464 | tf_op jit(solution)/shard_map/ppermute | solution.py:24
  223.5 0.9 collective-permute-start.30
  224.4 1.3 collective-permute-start.31
  225.7 0.7 maximum_select_fusion
  226.5 2.6 %collective-permute-done.30 = bf16[192,128]{1,0:T(8,128)(2,1)S(1)} collective-permute-done((bf16[192,128]{1,0:T(8,128)(2,1)S(1)}, bf16[192,128]{1,0:T(8,128)(2,1)S(1)}, u32[]{:S(2)}, u32[]{:S(2)}) %collective-permute-start.30) | collective-permute-done | bytes 49184 | tf_op jit(solution)/shard_map/ppermute | solution.py:24
  (62 shorter events, 10.3 us)
Async XLA Ops:
  1.6 10.2 %collective-permute-start.12 = (bf16[384,128]{1,0:T(8,128)(2,1)S(1)}, bf16[384,128]{1,0:T(8,128)(2,1)S(1)}, u32[]{:S(2)}, u32[]{:S(2)}) collective-permute-start(bf16[384,128]{1,0:T(8,128)(2,1)S(1)} %get-tuple-element.46), channel_id=1, source_target_pairs={{0,4},{4,0},{1,5},{5,1},{2,6},{6,2},{3,7},{7,3},{8,12},{12,8},{9,1... | collective-permute-start | bytes 294920 | tf_op jit(solution)/shard_map/ppermute | solution.py:28
  13.1 7.6 %copy-start.1 = (bf16[768,128]{1,0:T(8,128)(2,1)S(1)}, bf16[768,128]{1,0:T(8,128)(2,1)}, u32[]{:S(2)}) copy-start(bf16[768,128]{1,0:T(8,128)(2,1)} %param.4) | copy-start | bytes 589828
  13.1 80.0 %all-to-all-start = ((bf16[16,2,384,128]{3,2,1,0:T(8,128)(2,1)}), bf16[16,2,384,128]{3,2,1,0:T(8,128)(2,1)S(1)}, u32[]{:S(2)}, u32[]{:S(2)}) async-start(bf16[16,2,384,128]{3,2,1,0:T(8,128)(2,1)} %shard_map.51), calls=%async_computation | async-start | bytes 6291456 | tf_op jit(solution)/shard_map/all_to_all | solution.py:319
  20.8 36.3 %collective-permute-start = (bf16[192,128]{1,0:T(8,128)(2,1)S(1)}, bf16[192,128]{1,0:T(8,128)(2,1)S(1)}, u32[]{:S(2)}, u32[]{:S(2)}) collective-permute-start(bf16[192,128]{1,0:T(8,128)(2,1)S(1)} %get-tuple-element.50), channel_id=1, source_target_pairs={{0,1},{1,2},{2,3},{3,0},{4,5},{5,6},{6,7},{7,4},{8,9},{9,10},{10,1... | collective-permute-start | bytes 147464 | tf_op jit(solution)/shard_map/ppermute | solution.py:24
  22.3 34.8 %collective-permute-start.1 = (bf16[192,128]{1,0:T(8,128)(2,1)S(1)}, bf16[192,128]{1,0:T(8,128)(2,1)S(1)}, u32[]{:S(2)}, u32[]{:S(2)}) collective-permute-start(bf16[192,128]{1,0:T(8,128)(2,1)S(1)} %get-tuple-element.52), channel_id=1, source_target_pairs={{0,2},{1,3},{2,0},{3,1},{4,6},{5,7},{6,4},{7,5},{8,10},{9,11},{10,... | collective-permute-start | bytes 147464 | tf_op jit(solution)/shard_map/ppermute | solution.py:24
  25.0 33.4 %collective-permute-start.2 = (bf16[192,128]{1,0:T(8,128)(2,1)S(1)}, bf16[192,128]{1,0:T(8,128)(2,1)S(1)}, u32[]{:S(2)}, u32[]{:S(2)}) collective-permute-start(bf16[192,128]{1,0:T(8,128)(2,1)S(1)} %get-tuple-element.51), channel_id=1, source_target_pairs={{0,3},{1,0},{2,1},{3,2},{4,7},{5,4},{6,5},{7,6},{8,11},{9,8},{10,9... | collective-permute-start | bytes 147464 | tf_op jit(solution)/shard_map/ppermute | solution.py:24
  59.1 9.3 %collective-permute-start.3 = (bf16[192,512]{1,0:T(8,128)(2,1)S(1)}, bf16[192,512]{1,0:T(8,128)(2,1)S(1)}, u32[]{:S(2)}, u32[]{:S(2)}) collective-permute-start(bf16[192,512]{1,0:T(8,128)(2,1)S(1)} %get-tuple-element.47), channel_id=1, source_target_pairs={{0,64},{64,128},{128,192},{192,4},{4,68},{68,132},{132,196},{196,0... | collective-permute-start | bytes 589832 | tf_op jit(solution)/shard_map/ppermute | solution.py:20
  62.1 6.3 %collective-permute-start.4 = (bf16[192,512]{1,0:T(8,128)(2,1)S(1)}, bf16[192,512]{1,0:T(8,128)(2,1)S(1)}, u32[]{:S(2)}, u32[]{:S(2)}) collective-permute-start(bf16[192,512]{1,0:T(8,128)(2,1)S(1)} %get-tuple-element.47), channel_id=1, source_target_pairs={{0,196},{64,0},{128,64},{192,128},{4,192},{68,4},{132,68},{196,132... | collective-permute-start | bytes 589832 | tf_op jit(solution)/shard_map/ppermute | solution.py:20
  68.4 6.9 %collective-permute-start.5 = (bf16[192,512]{1,0:T(8,128)(2,1)S(1)}, bf16[192,512]{1,0:T(8,128)(2,1)S(1)}, u32[]{:S(2)}, u32[]{:S(2)}) collective-permute-start(bf16[192,512]{1,0:T(8,128)(2,1)S(1)} %collective-permute-done.3), channel_id=1, source_target_pairs={{0,64},{64,128},{128,192},{192,4},{4,68},{68,132},{132,196},{196,0... | collective-permute-start | bytes 589832 | tf_op jit(solution)/shard_map/ppermute | solution.py:20
  68.4 6.9 %collective-permute-start.6 = (bf16[192,512]{1,0:T(8,128)(2,1)S(1)}, bf16[192,512]{1,0:T(8,128)(2,1)S(1)}, u32[]{:S(2)}, u32[]{:S(2)}) collective-permute-start(bf16[192,512]{1,0:T(8,128)(2,1)S(1)} %collective-permute-done.4), channel_id=1, source_target_pairs={{0,196},{64,0},{128,64},{192,128},{4,192},{68,4},{132,68},{196,132... | collective-permute-start | bytes 589832 | tf_op jit(solution)/shard_map/ppermute | solution.py:20
  75.3 6.9 %collective-permute-start.7 = (bf16[192,512]{1,0:T(8,128)(2,1)S(1)}, bf16[192,512]{1,0:T(8,128)(2,1)S(1)}, u32[]{:S(2)}, u32[]{:S(2)}) collective-permute-start(bf16[192,512]{1,0:T(8,128)(2,1)S(1)} %collective-permute-done.5), channel_id=1, source_target_pairs={{0,64},{64,128},{128,192},{192,4},{4,68},{68,132},{132,196},{196,0... | collective-permute-start | bytes 589832 | tf_op jit(solution)/shard_map/ppermute | solution.py:20
  75.3 7.0 %collective-permute-start.8 = (bf16[192,512]{1,0:T(8,128)(2,1)S(1)}, bf16[192,512]{1,0:T(8,128)(2,1)S(1)}, u32[]{:S(2)}, u32[]{:S(2)}) collective-permute-start(bf16[192,512]{1,0:T(8,128)(2,1)S(1)} %collective-permute-done.6), channel_id=1, source_target_pairs={{0,196},{64,0},{128,64},{192,128},{4,192},{68,4},{132,68},{196,132... | collective-permute-start | bytes 589832 | tf_op jit(solution)/shard_map/ppermute | solution.py:20
  82.2 5.9 %collective-permute-start.9 = (bf16[96,512]{1,0:T(8,128)(2,1)S(1)}, bf16[96,512]{1,0:T(8,128)(2,1)S(1)}, u32[]{:S(2)}, u32[]{:S(2)}) collective-permute-start(bf16[96,512]{1,0:T(8,128)(2,1)S(1)} %slice.68), channel_id=1, source_target_pairs={{0,64},{64,128},{128,192},{192,4},{4,68},{68,132},{132,196},{196,0... | collective-permute-start | bytes 294920 | tf_op jit(solution)/shard_map/ppermute | solution.py:20
  82.3 6.4 %collective-permute-start.10 = (bf16[96,512]{1,0:T(8,128)(2,1)S(1)}, bf16[96,512]{1,0:T(8,128)(2,1)S(1)}, u32[]{:S(2)}, u32[]{:S(2)}) collective-permute-start(bf16[96,512]{1,0:T(8,128)(2,1)S(1)} %slice.69), channel_id=1, source_target_pairs={{0,196},{64,0},{128,64},{192,128},{4,192},{68,4},{132,68},{196,132... | collective-permute-start | bytes 294920 | tf_op jit(solution)/shard_map/ppermute | solution.py:20
  89.4 3.8 %collective-permute-start.11 = (bf16[8,192,512]{2,1,0:T(8,128)(2,1)}, bf16[8,192,512]{2,1,0:T(8,128)(2,1)}, u32[]{:S(2)}, u32[]{:S(2)}) collective-permute-start(bf16[8,192,512]{2,1,0:T(8,128)(2,1)} %bitcast.5.refs_1_), channel_id=1, source_target_pairs={{0,8},{8,0},{1,9},{9,1},{2,10},{10,2},{3,11},{11,3},{4,12},{12,4},... | collective-permute-start | bytes 4718600 | tf_op jit(solution)/shard_map/ppermute | solution.py:28
  89.7 19.5 %copy-start.2 = (s32[768]{0:T(1024)S(1)}, s32[768]{0:T(1024)}, u32[]{:S(2)}) copy-start(s32[768]{0:T(1024)} %param.5) | copy-start | bytes 9220
  102.3 7.0 %collective-permute-start.13 = (f32[8,384]{1,0:T(8,128)S(1)}, f32[8,384]{1,0:T(8,128)S(1)}, u32[]{:S(2)}, u32[]{:S(2)}) collective-permute-start(f32[8,384]{1,0:T(8,128)S(1)} %get-tuple-element.19), channel_id=1, source_target_pairs={{0,1},{1,2},{2,3},{3,0},{4,5},{5,6},{6,7},{7,4},{8,9},{9,10},{10,1... | collective-permute-start | bytes 36872 | tf_op jit(solution)/shard_map/ppermute | solution.py:24
  102.4 8.3 %collective-permute-start.14 = (f32[8,384]{1,0:T(8,128)S(1)}, f32[8,384]{1,0:T(8,128)S(1)}, u32[]{:S(2)}, u32[]{:S(2)}) collective-permute-start(f32[8,384]{1,0:T(8,128)S(1)} %get-tuple-element.19), channel_id=1, source_target_pairs={{0,2},{1,3},{2,0},{3,1},{4,6},{5,7},{6,4},{7,5},{8,10},{9,11},{10,... | collective-permute-start | bytes 36872 | tf_op jit(solution)/shard_map/ppermute | solution.py:24
  108.9 3.7 %collective-permute-start.15 = (f32[8,384]{1,0:T(8,128)S(1)}, f32[8,384]{1,0:T(8,128)S(1)}, u32[]{:S(2)}, u32[]{:S(2)}) collective-permute-start(f32[8,384]{1,0:T(8,128)S(1)} %get-tuple-element.19), channel_id=1, source_target_pairs={{0,3},{1,0},{2,1},{3,2},{4,7},{5,4},{6,5},{7,6},{8,11},{9,8},{10,9... | collective-permute-start | bytes 36872 | tf_op jit(solution)/shard_map/ppermute | solution.py:24
  112.6 6.4 %collective-permute-start.16 = (f32[9,384]{1,0:T(8,128)S(1)}, f32[9,384]{1,0:T(8,128)S(1)}, u32[]{:S(2)}, u32[]{:S(2)}) collective-permute-start(f32[9,384]{1,0:T(8,128)S(1)} %pad_maximum_fusion.2.refs_0_), channel_id=1, source_target_pairs={{0,16},{16,32},{32,48},{48,0},{1,17},{17,33},{33,49},{49,1},{2,18}... | collective-permute-start | bytes 41480 | tf_op jit(solution)/shard_map/ppermute | solution.py:24
  114.6 6.1 %collective-permute-start.17 = (f32[9,384]{1,0:T(8,128)S(1)}, f32[9,384]{1,0:T(8,128)S(1)}, u32[]{:S(2)}, u32[]{:S(2)}) collective-permute-start(f32[9,384]{1,0:T(8,128)S(1)} %pad_maximum_fusion.2.refs_0_), channel_id=1, source_target_pairs={{0,32},{16,48},{32,0},{48,16},{1,33},{17,49},{33,1},{49,17},{2,34}... | collective-permute-start | bytes 41480 | tf_op jit(solution)/shard_map/ppermute | solution.py:24
  118.6 3.8 %collective-permute-start.18 = (f32[9,384]{1,0:T(8,128)S(1)}, f32[9,384]{1,0:T(8,128)S(1)}, u32[]{:S(2)}, u32[]{:S(2)}) collective-permute-start(f32[9,384]{1,0:T(8,128)S(1)} %pad_maximum_fusion.2.refs_0_), channel_id=1, source_target_pairs={{0,48},{16,0},{32,16},{48,32},{1,49},{17,1},{33,17},{49,33},{2,50}... | collective-permute-start | bytes 41480 | tf_op jit(solution)/shard_map/ppermute | solution.py:24
  134.8 6.3 %collective-permute-start.20 = (f32[768,1024]{1,0:T(8,128)}, f32[768,1024]{1,0:T(8,128)}, u32[]{:S(2)}, u32[]{:S(2)}) collective-permute-start(f32[768,1024]{1,0:T(8,128)} %get-tuple-element.24), channel_id=1, source_target_pairs={{0,8},{8,0},{1,9},{9,1},{2,10},{10,2},{3,11},{11,3},{4,12},{12,4},... | collective-permute-start | bytes 9437192 | tf_op jit(solution)/shard_map/ppermute | solution.py:28
  134.9 50.6 %all-to-all-start.1 = ((bf16[16,2,384,128]{3,2,1,0:T(8,128)(2,1)}), bf16[16,2,384,128]{3,2,1,0:T(8,128)(2,1)S(1)}, u32[]{:S(2)}, u32[]{:S(2)}) async-start(bf16[16,2,384,128]{3,2,1,0:T(8,128)(2,1)} %get-tuple-element.22), calls=%async_computation.1 | async-start | bytes 6291456 | tf_op jit(solution)/shard_map/all_to_all | solution.py:344
  145.9 46.1 %collective-permute-start.21 = (bf16[192,512]{1,0:T(8,128)(2,1)}, bf16[192,512]{1,0:T(8,128)(2,1)S(1)}, u32[]{:S(2)}, u32[]{:S(2)}) collective-permute-start(bf16[192,512]{1,0:T(8,128)(2,1)} %get-tuple-element.26), channel_id=1, source_target_pairs={{0,196},{64,0},{128,64},{192,128},{4,192},{68,4},{132,68},{196,132... | collective-permute-start | bytes 589832 | tf_op jit(solution)/shard_map/ppermute | solution.py:20
  148.6 43.3 %collective-permute-start.22 = (bf16[192,512]{1,0:T(8,128)(2,1)}, bf16[192,512]{1,0:T(8,128)(2,1)}, u32[]{:S(2)}, u32[]{:S(2)}) collective-permute-start(bf16[192,512]{1,0:T(8,128)(2,1)} %get-tuple-element.27), channel_id=1, source_target_pairs={{0,132},{64,196},{128,0},{192,64},{4,128},{68,192},{132,4},{196,68... | collective-permute-start | bytes 589832 | tf_op jit(solution)/shard_map/ppermute | solution.py:20
  149.2 42.8 %collective-permute-start.23 = (bf16[96,512]{1,0:T(8,128)(2,1)}, bf16[96,512]{1,0:T(8,128)(2,1)}, u32[]{:S(2)}, u32[]{:S(2)}) collective-permute-start(bf16[96,512]{1,0:T(8,128)(2,1)} %get-tuple-element.28), channel_id=1, source_target_pairs={{0,68},{64,132},{128,196},{192,0},{4,64},{68,128},{132,192},{196,4... | collective-permute-start | bytes 294920 | tf_op jit(solution)/shard_map/ppermute | solution.py:20
  186.0 32.5 %copy-start = (f32[192,512]{1,0:T(8,128)S(1)}, f32[192,512]{1,0:T(8,128)}, u32[]{:S(2)}) copy-start(f32[192,512]{1,0:T(8,128)} %get-tuple-element.25) | copy-start | bytes 1179652
  186.0 19.1 %collective-permute-start.25 = (bf16[192,512]{1,0:T(8,128)(2,1)}, bf16[192,512]{1,0:T(8,128)(2,1)S(1)}, u32[]{:S(2)}, u32[]{:S(2)}) collective-permute-start(bf16[192,512]{1,0:T(8,128)(2,1)} %get-tuple-element.30), channel_id=1, source_target_pairs={{0,64},{64,128},{128,192},{192,4},{4,68},{68,132},{132,196},{196,0... | collective-permute-start | bytes 589832 | tf_op jit(solution)/shard_map/ppermute | solution.py:20
  186.1 21.0 %collective-permute-start.26 = (bf16[192,512]{1,0:T(8,128)(2,1)}, bf16[192,512]{1,0:T(8,128)(2,1)S(1)}, u32[]{:S(2)}, u32[]{:S(2)}) collective-permute-start(bf16[192,512]{1,0:T(8,128)(2,1)} %get-tuple-element.31), channel_id=1, source_target_pairs={{0,128},{64,192},{128,4},{192,68},{4,132},{68,196},{132,0},{196,64... | collective-permute-start | bytes 589832 | tf_op jit(solution)/shard_map/ppermute | solution.py:20
  192.0 13.2 %collective-permute-start.27 = (bf16[96,512]{1,0:T(8,128)(2,1)}, bf16[96,512]{1,0:T(8,128)(2,1)S(1)}, u32[]{:S(2)}, u32[]{:S(2)}) collective-permute-start(bf16[96,512]{1,0:T(8,128)(2,1)} %get-tuple-element.32), channel_id=1, source_target_pairs={{0,192},{64,4},{128,68},{192,132},{4,196},{68,0},{132,64},{196,128... | collective-permute-start | bytes 294920 | tf_op jit(solution)/shard_map/ppermute | solution.py:20
  193.2 25.3 %collective-permute-start.24 = (bf16[192,512]{1,0:T(8,128)(2,1)S(1)}, bf16[192,512]{1,0:T(8,128)(2,1)S(1)}, u32[]{:S(2)}, u32[]{:S(2)}) collective-permute-start(bf16[192,512]{1,0:T(8,128)(2,1)S(1)} %add_convert_fusion.2), channel_id=1, source_target_pairs={{0,196},{64,0},{128,64},{192,128},{4,192},{68,4},{132,68},{196,132... | collective-permute-start | bytes 589832 | tf_op jit(solution)/shard_map/ppermute | solution.py:20
  208.2 10.3 %collective-permute-start.28 = (bf16[192,512]{1,0:T(8,128)(2,1)S(1)}, bf16[192,512]{1,0:T(8,128)(2,1)S(1)}, u32[]{:S(2)}, u32[]{:S(2)}) collective-permute-start(bf16[192,512]{1,0:T(8,128)(2,1)S(1)} %add_convert_fusion.1), channel_id=1, source_target_pairs={{0,64},{64,128},{128,192},{192,4},{4,68},{68,132},{132,196},{196,0... | collective-permute-start | bytes 589832 | tf_op jit(solution)/shard_map/ppermute | solution.py:20
  212.0 13.7 %collective-permute-start.19 = (bf16[384,128]{1,0:T(8,128)(2,1)S(1)}, bf16[384,128]{1,0:T(8,128)(2,1)S(1)}, u32[]{:S(2)}, u32[]{:S(2)}) collective-permute-start(bf16[384,128]{1,0:T(8,128)(2,1)S(1)} %get-tuple-element.44), channel_id=1, source_target_pairs={{0,4},{4,0},{1,5},{5,1},{2,6},{6,2},{3,7},{7,3},{8,12},{12,8},{9,1... | collective-permute-start | bytes 294920 | tf_op jit(solution)/shard_map/ppermute | solution.py:28
  218.6 7.9 %collective-permute-start.29 = (bf16[192,128]{1,0:T(8,128)(2,1)S(1)}, bf16[192,128]{1,0:T(8,128)(2,1)S(1)}, u32[]{:S(2)}, u32[]{:S(2)}) collective-permute-start(bf16[192,128]{1,0:T(8,128)(2,1)S(1)} %get-tuple-element.40), channel_id=1, source_target_pairs={{0,3},{1,0},{2,1},{3,2},{4,7},{5,4},{6,5},{7,6},{8,11},{9,8},{10,9... | collective-permute-start | bytes 147464 | tf_op jit(solution)/shard_map/ppermute | solution.py:24
  223.5 5.6 %collective-permute-start.30 = (bf16[192,128]{1,0:T(8,128)(2,1)S(1)}, bf16[192,128]{1,0:T(8,128)(2,1)S(1)}, u32[]{:S(2)}, u32[]{:S(2)}) collective-permute-start(bf16[192,128]{1,0:T(8,128)(2,1)S(1)} %get-tuple-element.42), channel_id=1, source_target_pairs={{0,2},{1,3},{2,0},{3,1},{4,6},{5,7},{6,4},{7,5},{8,10},{9,11},{10,... | collective-permute-start | bytes 147464 | tf_op jit(solution)/shard_map/ppermute | solution.py:24
  224.4 5.3 %collective-permute-start.31 = (bf16[192,128]{1,0:T(8,128)(2,1)S(1)}, bf16[192,128]{1,0:T(8,128)(2,1)S(1)}, u32[]{:S(2)}, u32[]{:S(2)}) collective-permute-start(bf16[192,128]{1,0:T(8,128)(2,1)S(1)} %get-tuple-element.41), channel_id=1, source_target_pairs={{0,1},{1,2},{2,3},{3,0},{4,5},{5,6},{6,7},{7,4},{8,9},{9,10},{10,1... | collective-permute-start | bytes 147464 | tf_op jit(solution)/shard_map/ppermute | solution.py:24
